TPU v7x, 32 devices: a whole 2x2x4 slice. The times are simulated.
32 devices in a mesh: pool: 32 (over z, y, x, core).
Axes of the slice: x: 2, y: 2, z: 4, core: 2. Of those that a mesh axis runs over, the one named last changes fastest.
Arguments:
- queries: bfloat16 [256, 32, 32, 128], P('pool')
- k_new: bfloat16 [256, 32, 8, 128], P('pool')
- v_new: bfloat16 [256, 32, 8, 128], P('pool')
- k_pool: bfloat16 [8192, 16, 8, 128], P('pool')
- v_pool: bfloat16 [8192, 16, 8, 128], P('pool')
- block_table: int32 [256, 64], replicated
- write_ids: int32 [256, 2], P('pool')
Outputs:
- output 1: bfloat16 [256, 32, 32, 128], P('pool')
- output 2: bfloat16 [8192, 16, 8, 128], P('pool')
- output 3: bfloat16 [8192, 16, 8, 128], P('pool')
All inputs are finite; a program needn't handle non-finite values.
Results may differ from a plain program's by a relative error of at most 0.0108546.
Values are sent between devices in bfloat16 or wider.
A program may use at most 1 GiB of HBM per device.

v0:
```python
import jax
import jax.numpy as jnp
from jax import lax
from jax.sharding import PartitionSpec as P


def chunk_attention(q_grp, k_pref, v_pref, k_chunk, v_chunk):
    chunk_len = q_grp.shape[1]
    score_scale = q_grp.shape[-1] ** -0.5
    s_pref = jnp.einsum('rcgqd,rtgd->rcgqt', q_grp, k_pref, preferred_element_type=jnp.float32) * score_scale
    s_self = jnp.einsum('rcgqd,rtgd->rcgqt', q_grp, k_chunk, preferred_element_type=jnp.float32) * score_scale
    causal = (jnp.arange(chunk_len)[:, None] >= jnp.arange(chunk_len)[None, :])[None, :, None, None, :]
    s_self = jnp.where(causal, s_self, -jnp.inf)
    row_max = jnp.maximum(jnp.max(s_pref, axis=-1), jnp.max(s_self, axis=-1))[..., None]
    e_pref = jnp.exp(s_pref - row_max)
    e_self = jnp.exp(s_self - row_max)
    prob_total = jnp.sum(e_pref, axis=-1, keepdims=True) + jnp.sum(e_self, axis=-1, keepdims=True)
    p_pref = (e_pref / prob_total).astype(jnp.bfloat16)
    p_self = (e_self / prob_total).astype(jnp.bfloat16)
    attn_acc = jnp.einsum('rcgqt,rtgd->rcgqd', p_pref, v_pref, preferred_element_type=jnp.float32)
    return attn_acc + jnp.einsum('rcgqt,rtgd->rcgqd', p_self, v_chunk, preferred_element_type=jnp.float32)


def solution(mesh):
    n_dev = mesh.shape['pool']

    def local_step(queries, k_new, v_new, k_pool, v_pool, block_table, write_ids):
        req_count, chunk_len, q_heads, head_dim = queries.shape
        kv_heads = k_new.shape[2]
        per_dev, block_len = k_pool.shape[0], k_pool.shape[1]
        n_pref = block_table.shape[1]
        row_cap = 2 * n_pref // n_dev + (n_pref // 2 + n_dev - 1) // n_dev
        pair_cap = req_count * row_cap
        my_index = lax.axis_index('pool')
        owners = block_table // per_dev
        owned_here = (owners == my_index).reshape(n_dev, req_count * n_pref).astype(jnp.int32)
        send_slot = jnp.where(owned_here > 0, jnp.cumsum(owned_here, axis=1) - 1, pair_cap)
        dest_dev = jnp.broadcast_to(jnp.arange(n_dev)[:, None], send_slot.shape)
        local_ids = (block_table % per_dev).reshape(n_dev, req_count * n_pref)
        send_ids = jnp.zeros((n_dev, pair_cap), jnp.int32).at[dest_dev, send_slot].set(local_ids, mode='drop')
        k_recv = lax.all_to_all(k_pool[send_ids], 'pool', 0, 0, tiled=True)
        v_recv = lax.all_to_all(v_pool[send_ids], 'pool', 0, 0, tiled=True)
        my_owners = lax.dynamic_slice_in_dim(owners, my_index * req_count, req_count, 0).reshape(-1)
        from_owner = (my_owners[:, None] == jnp.arange(n_dev)[None, :]).astype(jnp.int32)
        slot_rank = jnp.sum(from_owner * (jnp.cumsum(from_owner, axis=0) - 1), axis=1)
        recv_idx = (my_owners * pair_cap + slot_rank).reshape(req_count, n_pref)
        flat_shape = (n_dev * pair_cap, block_len, kv_heads, head_dim)
        prefix_shape = (req_count, n_pref * block_len, kv_heads, head_dim)
        k_pref = k_recv.reshape(flat_shape)[recv_idx].reshape(prefix_shape)
        v_pref = v_recv.reshape(flat_shape)[recv_idx].reshape(prefix_shape)
        q_grp = queries.reshape(req_count, chunk_len, kv_heads, q_heads // kv_heads, head_dim)
        attn_acc = chunk_attention(q_grp, k_pref, v_pref, k_new, v_new)
        attn_out = attn_acc.reshape(req_count, chunk_len, q_heads, head_dim).astype(jnp.bfloat16)
        new_shape = (req_count * chunk_len // block_len, block_len, kv_heads, head_dim)
        targets = write_ids.reshape(-1)
        k_pool_out = k_pool.at[targets].set(k_new.reshape(new_shape))
        v_pool_out = v_pool.at[targets].set(v_new.reshape(new_shape))
        return attn_out, k_pool_out, v_pool_out

    row_spec = P('pool')
    return jax.shard_map(local_step, mesh=mesh, in_specs=(row_spec, row_spec, row_spec, row_spec, row_spec, P(), row_spec), out_specs=(row_spec, row_spec, row_spec), check_vma=False)
```

profile of v0, /device:TPU:5, one launch (start us, length us, event | category | flops | bytes accessed | tf_op | source)
XLA Modules:
  0.0 2047.9 jit_solution(10263728364195038571)
XLA Ops:
  0.6 0.0 copy-start
  0.6 10.7 copy.76
  11.3 0.0 copy-start.4
  11.3 0.0 copy-start.7
  11.3 0.0 copy-start.6
  11.3 10.5 copy.75
  21.9 0.0 copy-done.4
  21.9 0.1 copy.17
  22.0 0.1 add_select_fusion
  22.0 0.1 reshape.248
  22.1 0.1 broadcast_compare_fusion
  22.2 0.1 gt.14
  22.3 0.1 reshape.197
  22.4 1.2 reduce-window.14
  23.6 0.2 slice_reduce_fusion.1
  23.9 0.1 add_add_fusion
  24.1 0.0 copy-done.7
  24.1 0.1 and_reduce_fusion
  24.2 0.0 copy-done.6
  24.2 0.1 multiply_reduce_fusion
  24.3 60.3 %scatter_custom_fusion.2 = s32[1280]{0:T(1024)S(1)} fusion(s32[16384]{0:T(1024)S(1)} %bitcast.77, s32[16384]{0:T(1024)S(1)} %reshape.248, s32[]{:T(128)} %constant.28.clone.1), kind=kCustom, calls=%fused_computation.60 | custom fusion | bytes 5124
  84.7 0.1 reshape.196
  84.8 0.1 reshape.200
  84.9 31.0 %gather_fusion = bf16[1280,16,8,128]{3,2,1,0:T(8,128)(2,1)} fusion(bf16[256,16,8,128]{3,2,1,0:T(8,128)(2,1)} %copy.76, s32[2048]{0:T(1024)S(1)} %pad_clamp_fusion), kind=kCustom, calls=%fused_computation | custom fusion | bytes 83891200 | tf_op jit(solution)/shard_map/gather | solution.py:42
  115.9 6.7 all-to-all-start
  122.6 31.0 %gather_fusion.2 = bf16[1280,16,8,128]{3,2,1,0:T(8,128)(2,1)} fusion(bf16[256,16,8,128]{3,2,1,0:T(8,128)(2,1)} %copy.75, s32[2048]{0:T(1024)S(1)} %pad_clamp_fusion), kind=kCustom, calls=%fused_computation.2 | custom fusion | bytes 83891200 | tf_op jit(solution)/shard_map/gather | solution.py:41
  153.6 886.6 %all-to-all-done = bf16[32,40,16,8,128]{4,3,2,1,0:T(8,128)(2,1)} async-done(((bf16[32,40,16,8,128]{4,3,2,1,0:T(8,128)(2,1)}), bf16[32,40,16,8,128]{4,3,2,1,0:T(8,128)(2,1)}, u32[]{:S(2)}, u32[]{:S(2)}) %all-to-all-start) | async-done | bytes 41943072 | tf_op jit(solution)/shard_map/all_to_all | solution.py:42
  1040.1 0.0 copy-start.5
  1040.1 0.0 copy-start.3
  1040.1 0.0 copy-start.2
  1040.1 4.5 all-to-all-start.1
  1044.7 0.1 eq.35
  1044.8 0.1 eq.39
  1044.8 0.0 copy-done.5
  1044.8 0.1 copy.31
  1044.9 0.1 reshape.190
  1045.0 1.2 reduce-window.16
  1046.2 0.2 slice_reduce_fusion
  1046.4 0.1 fusion.21
  1046.5 0.1 reduce_sum.30
  1046.6 0.1 reshape.208
  1046.7 0.0 copy-done.3
  1046.7 2.6 scatter_fusion.1
  1049.3 0.0 copy-done.2
  1049.3 2.6 scatter_fusion
  1051.9 0.0 copy-done
  1051.9 5.5 fusion.8
  1057.3 14.4 gather_fusion.1
  1071.8 891.9 %all-to-all-done.1 = bf16[32,40,16,8,128]{4,3,2,1,0:T(8,128)(2,1)} async-done(((bf16[32,40,16,8,128]{4,3,2,1,0:T(8,128)(2,1)}), bf16[32,40,16,8,128]{4,3,2,1,0:T(8,128)(2,1)}, u32[]{:S(2)}, u32[]{:S(2)}) %all-to-all-start.1) | async-done | bytes 41943072 | tf_op jit(solution)/shard_map/all_to_all | solution.py:41
  1963.7 14.4 gather_fusion.3
  1978.1 0.0 copy-start.1
  1978.1 29.1 %bitcast_reduce_fusion = (f32[8,32,8,4]{1,3,2,0:T(4,128)S(1)}, f32[8,8,1024,32,4]{2,3,4,1,0:T(8,128)}) fusion(bf16[8,32,8,4,128]{4,3,2,1,0:T(4,128)(2,1)S(1)} %bitcast.66, bf16[8,1024,8,128,1]{3,2,1,0,4:T(8,128)(2,1)} %bitcast.70), kind=kOutput, calls=%fused_computation.8 | convolution fusion | flops 2164252672 | bytes 52461568 | tf_op jit(solution)/shard_map/rcgqd,rtgd->rcgqt/dot_general | solution.py:10
  2007.2 0.0 copy-done.1
  2007.2 1.5 fusion.7
  2008.8 14.3 fusion.1
  2023.1 3.3 fusion.11
  2026.5 19.3 fusion.6
  2045.8 2.1 copy.32
  (21 shorter events, 0.3 us)
Async XLA Ops:
  0.6 1051.2 %copy-start = (bf16[8,32,32,128]{3,2,1,0:T(8,128)(2,1)S(1)}, bf16[8,32,32,128]{3,2,1,0:T(8,128)(2,1)}, u32[]{:S(2)}) copy-start(bf16[8,32,32,128]{3,2,1,0:T(8,128)(2,1)} %param.7) | copy-start | bytes 6291460
  11.3 10.6 copy-start.4
  11.3 12.8 copy-start.7
  11.3 12.9 copy-start.6
  115.9 924.3 %all-to-all-start = ((bf16[32,40,16,8,128]{4,3,2,1,0:T(8,128)(2,1)}), bf16[32,40,16,8,128]{4,3,2,1,0:T(8,128)(2,1)}, u32[]{:S(2)}, u32[]{:S(2)}) async-start(bf16[32,40,16,8,128]{4,3,2,1,0:T(8,128)(2,1)} %bitcast.69), calls=%async_computation | async-start | bytes 83886080 | tf_op jit(solution)/shard_map/all_to_all | solution.py:42
  1040.1 4.7 copy-start.5
  1040.1 6.6 copy-start.3
  1040.1 9.2 copy-start.2
  1040.1 923.5 %all-to-all-start.1 = ((bf16[32,40,16,8,128]{4,3,2,1,0:T(8,128)(2,1)}), bf16[32,40,16,8,128]{4,3,2,1,0:T(8,128)(2,1)}, u32[]{:S(2)}, u32[]{:S(2)}) async-start(bf16[32,40,16,8,128]{4,3,2,1,0:T(8,128)(2,1)} %bitcast.68), calls=%async_computation.1 | async-start | bytes 83886080 | tf_op jit(solution)/shard_map/all_to_all | solution.py:41
  1978.1 29.1 %copy-start.1 = (f32[8,8,32,32,4]{3,2,4,1,0:T(8,128)S(1)}, f32[8,8,32,32,4]{3,2,4,1,0:T(8,128)}, u32[]{:S(2)}) copy-start(f32[8,8,32,32,4]{3,2,4,1,0:T(8,128)} %get-tuple-element.15) | copy-start | bytes 3145732
where the time goes:
time: 2050 us
  waiting for transfers between devices  1780 us (87%)
  local copies, waits for them, and re-layouts  181 us (9%)
  matrix products  57.2 us (3%)
    all_to_all x1, waiting for transfers between devices, local_step(): k_recv = lax.all_to_all(k_pool[send_ids], 'pool', 0, 0, tiled=True)  892 us
    all_to_all x1, waiting for transfers between devices, local_step(): v_recv = lax.all_to_all(v_pool[send_ids], 'pool', 0, 0, tiled=True)  887 us
    unnamed x23, local copies, waits for them, and re-layouts  83.9 us
  transfers between devices with their start and end apart: 2, of which 2 were waited for; matrix products, arithmetic and copies ran while one was open for 3% of the time, Pallas kernels for 0%

commit v1 on v0

v1 whole, which is shorter than its diff:
```python
import functools

import jax
import jax.numpy as jnp
from jax import lax
from jax.experimental import pallas as pl
from jax.experimental.pallas import tpu as pltpu
from jax.sharding import PartitionSpec as P

F32 = jnp.float32
BF16 = jnp.bfloat16
ROW_CAP = 5
POOL_CHUNK = 16
HOT_CAP = 64
MESH = pl.DeviceIdType.MESH


def any_spec():
    return pl.BlockSpec(memory_space=pl.ANY)


def smem_spec():
    return pl.BlockSpec(memory_space=pltpu.SMEM)


def vmem_spec():
    return pl.BlockSpec(memory_space=pltpu.VMEM)


def pack_pool_kernel(cfg, counts, near_ids, cross_ids, hot_ids, perm, k_pool, v_pool, x_near, x_cross, x_hot,
                     raw, head_major, zero, in_sem, out_sem, zero_sem):
    per_dev, n_half, pair_cap = cfg
    n_chunk = per_dev // POOL_CHUNK
    n_zero = HOT_CAP // POOL_CHUNK

    def chunk_copies(chunk, slot):
        rows = pl.ds(chunk * POOL_CHUNK, POOL_CHUNK)
        return (pltpu.make_async_copy(k_pool.at[rows], raw.at[slot, 0], in_sem.at[slot, 0]),
                pltpu.make_async_copy(v_pool.at[rows], raw.at[slot, 1], in_sem.at[slot, 1]))

    for copy in chunk_copies(0, 0):
        copy.start()
    zero[...] = jnp.zeros_like(zero)

    def turn_chunk(chunk, carry):
        slot = lax.rem(chunk, 2)

        @pl.when(chunk + 1 < n_chunk)
        def _():
            for copy in chunk_copies(chunk + 1, 1 - slot):
                copy.start()

        for copy in chunk_copies(chunk, slot):
            copy.wait()
        for j in range(POOL_CHUNK):
            both = jnp.concatenate([raw[slot, 0, j], raw[slot, 1, j]], axis=1)
            turned = jnp.dot(perm[...], both, preferred_element_type=F32).astype(BF16)
            head_major[chunk * POOL_CHUNK + j, 0:128, :] = turned[:, 0:128]
            head_major[chunk * POOL_CHUNK + j, 128:256, :] = turned[:, 128:256]

        @pl.when(chunk == 0)
        def _():
            for i in range(n_zero):
                pltpu.make_async_copy(zero, x_hot.at[pl.ds(i * POOL_CHUNK, POOL_CHUNK)], zero_sem.at[i]).start()
        return carry

    lax.fori_loop(0, n_chunk, turn_chunk, 0)

    def start_list(ids, row, count, dest, base):
        def body(k, carry):
            pltpu.make_async_copy(head_major.at[ids[row, k]], dest.at[base + k], out_sem).start()
            return carry
        lax.fori_loop(0, count, body, 0)

    start_list(cross_ids, 0, counts[n_half], x_cross, 0)
    total = counts[n_half] + counts[n_half + 1]
    for i in range(n_zero):
        pltpu.make_async_copy(zero, x_hot.at[pl.ds(i * POOL_CHUNK, POOL_CHUNK)], zero_sem.at[i]).wait()
    start_list(hot_ids, 0, counts[n_half + 1], x_hot, counts[n_half + 2])
    for q in range(n_half):
        start_list(near_ids, q, counts[q], x_near, q * pair_cap)
        total = total + counts[q]

    def drain(k, carry):
        pltpu.make_async_copy(head_major.at[0], x_near.at[0], out_sem).wait()
        return carry
    lax.fori_loop(0, total, drain, 0)


def pack_relay_kernel(cfg, counts, ids, arrived, x_out, stage, in_sem, out_sem):
    n_half, pair_cap, n_cross = cfg

    whole = pltpu.make_async_copy(arrived.at[pl.ds(0, n_cross)], stage, in_sem)
    whole.start()
    whole.wait()
    total = 0
    for q in range(n_half):
        def store(k, carry, q=q):
            pltpu.make_async_copy(stage.at[ids[q, k]], x_out.at[q * pair_cap + k], out_sem).start()
            return carry
        lax.fori_loop(0, counts[q], store, 0)
        total = total + counts[q]

    def drain(k, carry):
        pltpu.make_async_copy(stage.at[0], x_out.at[0], out_sem).wait()
        return carry
    lax.fori_loop(0, total, drain, 0)


def xor_bits(index, bits):
    out = index
    bit = 1
    while bit <= bits:
        if bits & bit:
            out = out + bit - 2 * bit * lax.rem(index // bit, 2)
        bit *= 2
    return out


def exchange_kernel(cfg, *refs):
    n_half, pair_cap, pair_send, n_cross, base = cfg
    if n_cross:
        x_near, x_cross, recv, arrived, own, send_sem, recv_sem, own_sem = refs
    else:
        x_near, _, recv, own, send_sem, recv_sem, own_sem = refs
    me = lax.axis_index('pool')
    in_half = lax.rem(me, n_half)
    half = me // n_half
    barrier = pltpu.get_barrier_semaphore()
    peers = [(j, half * n_half + xor_bits(in_half, j)) for j in range(1, n_half)]
    if n_cross:
        peers.append((n_half, (1 - half) * n_half + in_half))
    for _, peer in peers:
        pl.semaphore_signal(barrier, inc=1, device_id=(peer,), device_id_type=MESH)
    own_in = pltpu.make_async_copy(x_near.at[pl.ds(in_half * pair_cap, pair_send)], own, own_sem.at[0])
    own_in.start()
    pl.semaphore_wait(barrier, len(peers))
    copies = []
    for j, peer in reversed(peers):
        if j == n_half:
            src, dst = x_cross.at[pl.ds(0, n_cross)], arrived.at[pl.ds(0, n_cross)]
        else:
            src = x_near.at[pl.ds(xor_bits(in_half, j) * pair_cap, pair_send)]
            dst = recv.at[pl.ds((base + in_half) * pair_cap, pair_send)]
        copy = pltpu.make_async_remote_copy(
            src_ref=src, dst_ref=dst, send_sem=send_sem.at[j], recv_sem=recv_sem.at[j],
            device_id=(peer,), device_id_type=MESH)
        copy.start()
        copies.append(copy)
    own_in.wait()
    own_out = pltpu.make_async_copy(own, recv.at[pl.ds((base + in_half) * pair_cap, pair_send)], own_sem.at[1])
    own_out.start()
    own_out.wait()
    for copy in copies:
        copy.wait()


def attend_kernel(cfg, pos, q_ref, kn_ref, vn_ref, perm, recv, hot, out_ref, kv, heads_out, sem):
    n_pref, block_len, kv_heads, groups, chunk_len, head_dim, n_req, hot_base = cfg
    req = pl.program_id(0)
    slot = lax.rem(req, 2)
    exp_scale = float(head_dim ** -0.5 * 1.4426950408889634)

    def fetch(which, into):
        def body(k, carry):
            at = pos[which, k]

            @pl.when(at < hot_base)
            def _():
                pltpu.make_async_copy(recv.at[at], kv.at[into, k], sem.at[into]).start()

            @pl.when(at >= hot_base)
            def _():
                pltpu.make_async_copy(hot.at[at - hot_base], kv.at[into, k], sem.at[into]).start()
            return carry
        lax.fori_loop(0, n_pref, body, 0, unroll=8)

    @pl.when(req == 0)
    def _():
        fetch(0, 0)

    @pl.when(req + 1 < n_req)
    def _():
        fetch(req + 1, 1 - slot)

    pltpu.make_async_copy(recv.at[pl.ds(0, n_pref)], kv.at[slot], sem.at[slot]).wait()

    rows = chunk_len * groups
    token = lax.broadcasted_iota(jnp.int32, (rows, chunk_len), 0) // groups
    causal = lax.broadcasted_iota(jnp.int32, (rows, chunk_len), 1) <= token
    n_keys = n_pref * block_len
    nt = (((1,), (1,)), ((), ()))
    for h in range(kv_heads):
        q_h = q_ref[0, h]
        k_h = kv[slot, :, h * block_len:(h + 1) * block_len, :].reshape(n_keys, head_dim)
        v_at = (kv_heads + h) * block_len
        v_h = kv[slot, :, v_at:v_at + block_len, :].reshape(n_keys, head_dim)
        s_pref = lax.dot_general(q_h, k_h, nt, preferred_element_type=F32)
        s_self = lax.dot_general(q_h, kn_ref[0, h], nt, preferred_element_type=F32)
        s_self = jnp.where(causal, s_self, -jnp.inf)
        row_max = jnp.maximum(jnp.max(s_pref, axis=-1, keepdims=True), jnp.max(s_self, axis=-1, keepdims=True))
        e_pref = jnp.exp2((s_pref - row_max) * exp_scale)
        e_self = jnp.exp2((s_self - row_max) * exp_scale)
        total = jnp.sum(e_pref, axis=-1, keepdims=True) + jnp.sum(e_self, axis=-1, keepdims=True)
        inv = 1.0 / total
        p_pref = (e_pref * inv).astype(BF16)
        p_self = (e_self * inv).astype(BF16)
        acc = jnp.dot(p_pref, v_h, preferred_element_type=F32)
        acc = acc + jnp.dot(p_self, vn_ref[0, h], preferred_element_type=F32)
        heads_out[h] = acc.astype(BF16)
    span = 256 // kv_heads
    for g in range(rows // span):
        part = heads_out[:, g * span:(g + 1) * span, :].reshape(256, head_dim)
        out_ref[0, g * 256:(g + 1) * 256, :] = jnp.dot(perm[...], part, preferred_element_type=F32).astype(BF16)


def onehot(values, size):
    return (values[..., None] == jnp.arange(size, dtype=jnp.int32)).astype(BF16)


def ranks(ind):
    n = ind.shape[-1]
    strict = (jnp.arange(n)[:, None] < jnp.arange(n)[None, :]).astype(BF16)
    return jnp.einsum('...b,bk->...k', ind.astype(BF16), strict, preferred_element_type=F32).astype(jnp.int32)


def compact(ind, rank, value, size):
    hit = ind[..., :, None] & (rank[..., :, None] == jnp.arange(size))
    return jnp.sum(jnp.where(hit, value[..., :, None], 0), axis=-2)


def count(ind):
    return jnp.sum(ind.astype(jnp.int32), axis=-1)


def permutation(src_of_row):
    n = src_of_row.shape[0]
    return (src_of_row[:, None] == jnp.arange(n)[None, :]).astype(BF16)


def solution(mesh):
    n_dev = mesh.shape['pool']

    def local_step(queries, k_new, v_new, k_pool, v_pool, block_table, write_ids):
        req_count, chunk_len, q_heads, head_dim = queries.shape
        kv_heads = k_new.shape[2]
        groups = q_heads // kv_heads
        per_dev, block_len = k_pool.shape[0], k_pool.shape[1]
        n_pref = block_table.shape[1]
        block_rows = block_len * kv_heads
        pair_cap = req_count * ROW_CAP
        n_half = n_dev // 2
        hot_base = n_dev * pair_cap
        me = lax.axis_index('pool')
        half, partner = me // n_half, (me + n_half) % n_dev
        take = lambda x, at, axis: lax.dynamic_index_in_dim(x, at, axis, keepdims=False)

        table = block_table.reshape(n_dev, req_count * n_pref)
        want = jnp.einsum('deo,deb->dob', onehot(table // per_dev, n_dev), onehot(table % per_dev, per_dev),
                          preferred_element_type=F32) > 0
        popular = jnp.sum(want.astype(jnp.int32), axis=0)
        level_of = jnp.arange(2, n_dev + 2)
        at_least = jnp.sum((popular[None] >= level_of[:, None, None]).astype(jnp.int32), axis=(1, 2))
        threshold = 2 + jnp.sum((at_least > HOT_CAP).astype(jnp.int32))
        hot = popular >= threshold
        hot_count = count(hot)
        hot_start = jnp.cumsum(hot_count) - hot_count
        hot_rank = ranks(hot)
        rest = want & ~hot
        rank = ranks(rest)
        pair_count = count(rest)
        union = jnp.any(rest.reshape(2, n_half, n_dev, per_dev), axis=1)
        union_rank = ranks(union)
        union_count = count(union)
        other = (jnp.arange(2)[:, None] != jnp.arange(n_dev)[None, :] // n_half)
        pair_max = jnp.max(pair_count)
        union_max = jnp.max(jnp.where(other, union_count, 0))

        ids = jnp.arange(per_dev, dtype=jnp.int32)
        rest_half = lax.dynamic_slice_in_dim(rest, half * n_half, n_half, 0)
        rank_half = lax.dynamic_slice_in_dim(rank, half * n_half, n_half, 0)
        count_half = lax.dynamic_slice_in_dim(pair_count, half * n_half, n_half, 0)
        near_ids = compact(take(rest_half, me, 1), take(rank_half, me, 1), ids, pair_cap)
        relay_ids = compact(take(rest_half, partner, 1), take(rank_half, partner, 1),
                            take(take(union_rank, half, 0), partner, 0), pair_cap)
        cross_ids = compact(take(take(union, 1 - half, 0), me, 0), take(take(union_rank, 1 - half, 0), me, 0),
                            ids, per_dev)[None]
        hot_ids = compact(take(hot, me, 0), take(hot_rank, me, 0), ids, HOT_CAP)[None]
        counts = jnp.concatenate([take(count_half, me, 1), jnp.stack([
            union_count[1 - half, me], hot_count[me], hot_start[me]])])
        relay_counts = take(count_half, partner, 1)

        my_table = lax.dynamic_slice_in_dim(block_table, me * req_count, req_count, 0)
        owner = jnp.arange(n_dev)
        group = owner % n_half + jnp.where(owner // n_half == half, 0, n_half)
        place = jnp.where(hot, hot_base + hot_start[:, None] + hot_rank, group[:, None] * pair_cap + take(rank, me, 0))
        pos = place.reshape(-1)[my_table]

        block_shape = (2 * block_rows, head_dim)
        shaped = lambda n: jax.ShapeDtypeStruct((n,) + block_shape, BF16)
        row = jnp.arange(block_rows)
        turn = permutation((row % block_len) * kv_heads + row // block_len)
        x_near, x_cross, x_hot = pl.pallas_call(
            functools.partial(pack_pool_kernel, (per_dev, n_half, pair_cap)),
            out_shape=(shaped(n_half * pair_cap), shaped(per_dev), shaped(HOT_CAP)),
            in_specs=[smem_spec()] * 4 + [vmem_spec()] + [any_spec()] * 2,
            out_specs=(any_spec(),) * 3,
            scratch_shapes=[
                pltpu.VMEM((2, 2, POOL_CHUNK, block_rows, head_dim), BF16),
                pltpu.VMEM((per_dev,) + block_shape, BF16),
                pltpu.VMEM((POOL_CHUNK,) + block_shape, BF16),
                pltpu.SemaphoreType.DMA((2, 2)),
                pltpu.SemaphoreType.DMA,
                pltpu.SemaphoreType.DMA((HOT_CAP // POOL_CHUNK,)),
            ],
            compiler_params=pltpu.CompilerParams(vmem_limit_bytes=40 << 20),
            name='pack_pool',
        )(counts, near_ids, cross_ids, hot_ids, turn,
          k_pool.reshape(per_dev, block_rows, head_dim), v_pool.reshape(per_dev, block_rows, head_dim))

        rows = chunk_len * groups
        q_heads_major = queries.reshape(req_count, chunk_len, kv_heads, groups, head_dim)
        q_heads_major = q_heads_major.transpose(0, 2, 1, 3, 4).reshape(req_count, kv_heads, rows, head_dim)
        kn = k_new.transpose(0, 2, 1, 3)
        vn = v_new.transpose(0, 2, 1, 3)
        span_tok = 256 // q_heads
        out_row = jnp.arange(256)
        tok, head, grp = out_row // q_heads, (out_row % q_heads) // groups, out_row % groups
        back = permutation(head * (span_tok * groups) + tok * groups + grp)

        def exchange_and_attend(level, pair_send, n_cross, x_near, x_cross, x_hot, relay_counts, relay_ids, pos,
                                q_heads_major, kn, vn, back):
            hot_all = lax.psum(x_hot, 'pool')
            sems = [pltpu.VMEM((pair_send,) + block_shape, BF16), pltpu.SemaphoreType.DMA((n_half + 1,)),
                    pltpu.SemaphoreType.DMA((n_half + 1,)), pltpu.SemaphoreType.DMA((2,))]
            cost = lambda n: pl.CostEstimate(flops=n, bytes_accessed=1 << 20, transcendentals=0)
            recv, arrived = pl.pallas_call(
                functools.partial(exchange_kernel, (n_half, pair_cap, pair_send, n_cross, 0)),
                out_shape=(shaped(n_dev * pair_cap), shaped(n_cross)),
                in_specs=[any_spec()] * 2, out_specs=(any_spec(),) * 2, scratch_shapes=sems,
                compiler_params=pltpu.CompilerParams(collective_id=2 * level, has_side_effects=True,
                                                     vmem_limit_bytes=8 << 20),
                cost_estimate=cost(10 ** 10), name='exchange_near',
            )(x_near, x_cross)
            x_relay = pl.pallas_call(
                functools.partial(pack_relay_kernel, (n_half, pair_cap, n_cross)),
                out_shape=shaped(n_half * pair_cap),
                in_specs=[smem_spec()] * 2 + [any_spec()], out_specs=any_spec(),
                scratch_shapes=[pltpu.VMEM((n_cross,) + block_shape, BF16), pltpu.SemaphoreType.DMA,
                                pltpu.SemaphoreType.DMA],
                compiler_params=pltpu.CompilerParams(vmem_limit_bytes=24 << 20), name='pack_relay',
            )(relay_counts, relay_ids, arrived)
            recv = pl.pallas_call(
                functools.partial(exchange_kernel, (n_half, pair_cap, pair_send, 0, n_half)),
                out_shape=shaped(n_dev * pair_cap),
                in_specs=[any_spec()] * 2, out_specs=any_spec(), scratch_shapes=sems,
                input_output_aliases={1: 0},
                compiler_params=pltpu.CompilerParams(collective_id=2 * level + 1, has_side_effects=True,
                                                     vmem_limit_bytes=8 << 20),
                cost_estimate=cost(10 ** 10), name='exchange_far',
            )(x_relay, recv)
            cfg = (n_pref, block_len, kv_heads, groups, chunk_len, head_dim, req_count, hot_base)
            return pl.pallas_call(
                functools.partial(attend_kernel, cfg),
                out_shape=jax.ShapeDtypeStruct((req_count, chunk_len * q_heads, head_dim), BF16),
                grid=(req_count,),
                in_specs=[
                    smem_spec(),
                    pl.BlockSpec((1, kv_heads, rows, head_dim), lambda r: (r, 0, 0, 0)),
                    pl.BlockSpec((1, kv_heads, chunk_len, head_dim), lambda r: (r, 0, 0, 0)),
                    pl.BlockSpec((1, kv_heads, chunk_len, head_dim), lambda r: (r, 0, 0, 0)),
                    pl.BlockSpec((256, 256), lambda r: (0, 0)),
                    any_spec(), any_spec(),
                ],
                out_specs=pl.BlockSpec((1, chunk_len * q_heads, head_dim), lambda r: (r, 0, 0)),
                scratch_shapes=[
                    pltpu.VMEM((2, n_pref) + block_shape, BF16),
                    pltpu.VMEM((kv_heads, rows, head_dim), BF16),
                    pltpu.SemaphoreType.DMA((2,)),
                ],
                compiler_params=pltpu.CompilerParams(
                    vmem_limit_bytes=48 << 20, dimension_semantics=('arbitrary',)),
                name='attend',
            )(pos, q_heads_major, kn, vn, back, recv, hot_all)

        sizes = ((req_count, per_dev // 4), (req_count + req_count // 2, per_dev * 5 // 16), (pair_cap, per_dev))
        level = jnp.int32(0)
        for pair_send, n_cross in sizes[:-1]:
            level = level + ((pair_max > pair_send) | (union_max > n_cross)).astype(jnp.int32)
        attn = lax.switch(
            level, [functools.partial(exchange_and_attend, i, *s) for i, s in enumerate(sizes)],
            x_near, x_cross, x_hot, relay_counts, relay_ids, pos, q_heads_major, kn, vn, back)
        attn_out = attn.reshape(req_count, chunk_len, q_heads, head_dim)
        new_shape = (req_count * chunk_len // block_len, block_len, kv_heads, head_dim)
        targets = write_ids.reshape(-1)
        k_pool_out = k_pool.at[targets].set(k_new.reshape(new_shape))
        v_pool_out = v_pool.at[targets].set(v_new.reshape(new_shape))
        return attn_out, k_pool_out, v_pool_out

    row_spec = P('pool')
    return jax.shard_map(local_step, mesh=mesh, in_specs=(row_spec, row_spec, row_spec, row_spec, row_spec, P(), row_spec), out_specs=(row_spec, row_spec, row_spec), check_vma=False)
```

time: 2050 us -> 536 us (0.26)
  the two profiles are of different devices: /device:TPU:5 before, /device:TPU:0 now
where the time goes in v1:
time: 536 us; the launch traced here: 540 us
  Pallas kernels  405 us (76%)
  local copies, waits for them, and re-layouts  64.9 us (12%)
  waiting for transfers between devices  33.7 us (6%)
  between operations  17.4 us (3%)
  other arithmetic  12.9 us (2%)
    pallas_call x2, Pallas kernels, exchange_and_attend(): pl.pallas_call(functools.partial(exchange_kernel, (n_half, pair_cap, pair...  342 us
    pallas_call x1, Pallas kernels, exchange_and_attend(): pl.pallas_call(functools.partial(attend_kernel, cfg), out_shape=jax.Shape...  41.1 us
    psum x1, waiting for transfers between devices, exchange_and_attend(): hot_all = lax.psum(x_hot, 'pool')  33.2 us
    unnamed x35, local copies, waits for them, and re-layouts  30.2 us
    pallas_call x1, Pallas kernels, local_step(): pl.pallas_call(functools.partial(pack_pool_kernel, (per_dev, n_half, pair...  18.3 us
    cond x6, local copies, waits for them, and re-layouts  13.6 us
  transfers between devices with their start and end apart: 1, of which 1 were waited for; matrix products, arithmetic and copies ran while one was open for 2% of the time, Pallas kernels for 64%

profile of v1, /device:TPU:0, one launch (start us, length us, event | category | flops | bytes accessed | tf_op | source)
XLA Modules:
  0.0 539.8 jit_solution(11388464393222696042)
XLA Ops:
  7.2 10.5 %copy.148 = bf16[256,16,8,128]{3,2,1,0:T(8,128)(2,1)} copy(bf16[256,16,8,128]{3,2,1,0:T(8,128)(2,1)} %param.13) | data formatting | bytes 16777216
  17.7 10.5 %copy.149 = bf16[256,16,8,128]{3,2,1,0:T(8,128)(2,1)} copy(bf16[256,16,8,128]{3,2,1,0:T(8,128)(2,1)} %param.14) | data formatting | bytes 16777216
  28.2 0.1 copy.83
  28.3 0.1 reshape.303
  28.5 4.3 convert_reduce_fusion.2
  32.8 0.7 convert_reduce_fusion.1
  33.6 1.1 and_select_fusion.12
  35.4 0.1 convert_reduce_fusion.4
  35.5 0.2 bitcast_reduce_fusion
  35.7 0.6 convert_reduce_fusion
  36.3 0.6 copy-done.8
  36.9 0.2 dynamic-slice_reduce_fusion
  37.1 0.1 convert_reduce_fusion.3
  37.2 0.6 dynamic_slice.124
  37.8 0.1 copy.84
  38.0 0.1 reduce.1
  38.1 0.6 dynamic_slice.126
  38.7 0.7 dynamic_slice.125
  39.3 2.0 pad_add_fusion.counts
  41.4 0.3 convolution_convert_fusion
  41.8 0.1 copy.143
  41.9 0.8 copy-done.5
  42.7 1.4 select_reduce_fusion.3.near_ids
  44.1 0.2 convolution_convert_fusion.1
  44.3 0.6 copy-done.18
  45.0 0.2 select_reduce_fusion.4
  45.1 0.2 convolution_convert_fusion.2
  45.3 0.1 select_reduce_fusion.5
  45.4 0.1 fusion.27.perm
  45.5 0.3 copy-done.12
  45.9 3.4 copy-done.3
  49.3 18.3 %pack_pool.1 = (bf16[640,256,128]{2,1,0:T(8,128)(2,1)}, bf16[256,256,128]{2,1,0:T(8,128)(2,1)}, bf16[64,256,128]{2,1,0:T(8,128)(2,1)}) custom-call(s32[19]{0:T(128)S(1)} %pad_add_fusion.counts, s32[16,40]{1,0:T(8,128)S(1)} %select_reduce_fusion.3.near_ids, s32[1,256]{1,0:T(1,128)S(1)} %bitcast.125, s32[1,64]{1,0:T(1,128)S(1)} %bitcast.126, ...), custom_call_target="tpu_custom_call" | custom-call | tf_op jit(solution)/shard_map/pack_pool/pallas_call | solution.py:303
  67.5 1.6 copy_bitcast_fusion.3
  69.1 0.3 copy-done.4
  69.4 2.2 copy.85
  71.6 1.5 eq.176
  73.1 0.1 fusion.24
  73.3 1.6 broadcast_in_dim.117
  74.8 0.6 fusion.32
  76.0 0.7 reduce_max.18
  78.6 447.7 %conditional.1 = (bf16[8,32,32,128]{3,2,1,0:T(8,128)(2,1)}) conditional(s32[]{:T(128)} %clamp.59, (s32[32]{0:T(128)S(1)}, s32[32,1]{1,0:T(8,128)S(1)}, s32[32,256]{1,0:T(8,128)S(1)}, s32[32,1]{0,1:T(1,128)S(1)}, s32[32,1]{0,1:T(1,128)S(1)}, /*index=5*/s32[]{:T(128)}, s32[32,32,256]{2,1,0:T(8,128)}, s32[]{:T(128)}, ...), branch_computations={%region_13.16_spmd, %region_16.19_spmd, %region_19.22_spmd} | conditional | flops 20002779136 | bytes 201567488 | solution.py:390
  78.6 0.2 all-reduce.4.cloned.1.call-start
  78.8 0.5 all-reduce.4.cloned.1.call-update
  79.3 0.9 constant_dynamic-slice_fusion.1
  80.3 0.6 copy.119
  80.9 0.3 copy.92
  81.3 0.1 copy.88
  81.4 0.8 fusion.1
  82.3 0.1 copy.89
  82.4 0.1 reshape.315
  82.5 3.1 gather_fusion
  85.7 2.7 copy.90
  88.4 0.7 constant_dynamic-slice_fusion
  89.1 3.6 select_reduce_fusion.ids
  92.8 218.9 %exchange_near.3 = (bf16[1280,256,128]{2,1,0:T(8,128)(2,1)}, bf16[64,256,128]{2,1,0:T(8,128)(2,1)S(1)}) custom-call(bf16[640,256,128]{2,1,0:T(8,128)(2,1)} %get-tuple-element.622.refs_0_, bf16[256,256,128]{2,1,0:T(8,128)(2,1)} %get-tuple-element.623.refs_1_), custom_call_target="tpu_custom_call" | custom-call | flops 10000000000 | bytes 1048576 | tf_op jit(solution)/shard_map/cond/branch_0_fun/exchange_near/pallas_call | solution.py:337
  311.7 4.1 pack_relay.3.refs_0_
  315.8 13.0 %copy-done = bf16[640,256,128]{2,1,0:T(8,128)(2,1)S(1)} copy-done((bf16[640,256,128]{2,1,0:T(8,128)(2,1)S(1)}, bf16[640,256,128]{2,1,0:T(8,128)(2,1)}, u32[]{:S(2)}) %copy-start) | copy-done | bytes 41943064 | tf_op jit(solution)/shard_map/cond
  328.8 122.6 %exchange_far.3.recv = bf16[1280,256,128]{2,1,0:T(8,128)(2,1)} custom-call(bf16[640,256,128]{2,1,0:T(8,128)(2,1)S(1)} %copy-done, bf16[1280,256,128]{2,1,0:T(8,128)(2,1)} %get-tuple-element.625.refs_1_), custom_call_target="tpu_custom_call", output_to_operand_aliasing={{}: (1, {})} | custom-call | flops 10000000000 | bytes 1048576 | tf_op jit(solution)/shard_map/cond/branch_0_fun/exchange_far/pallas_call | solution.py:353
  451.4 33.2 %all-reduce.4.cloned.1.call-done.hot = bf16[64,256,128]{2,1,0:T(8,128)(2,1)} async-done(((bf16[64,256,128]{2,1,0:T(8,128)(2,1)}), bf16[64,256,128]{2,1,0:T(8,128)(2,1)}) %all-reduce.4.cloned.1.call-update) | async-done | bytes 4194320 | tf_op jit(solution)/shard_map/cond/branch_0_fun/psum | solution.py:333
  484.6 41.1 %attend.3 = bf16[8,1024,128]{2,1,0:T(8,128)(2,1)} custom-call(s32[8,64]{1,0:T(8,128)S(1)} %reshape.314.pos, bf16[8,8,128,128]{3,2,1,0:T(8,128)(2,1)S(1)} %bitcast.122, bf16[8,8,32,128]{3,2,1,0:T(8,128)(2,1)S(1)} %get-tuple-element.611.kn_ref, bf16[8,8,32,128]{3,2,1,0:T(8,128)(2,1)S(1)} %get-tuple-element.612.vn_ref, ...), custom_call_target="tpu_custom_call" | custom-call | tf_op jit(solution)/shard_map/cond/branch_0_fun/attend/pallas_call | solution.py:363
  526.3 0.8 copy.103
  527.1 0.1 reshape.310
  527.1 2.9 scatter_fusion
  530.0 2.9 scatter_fusion.1
  (49 shorter events, 0.7 us)
Async XLA Ops:
  17.7 10.5 %copy-start.6 = (s32[256,64]{0,1:T(8,128)S(1)}, s32[256,64]{0,1:T(8,128)}, u32[]{:S(2)}) copy-start(s32[256,64]{0,1:T(8,128)} %param.15) | copy-start | bytes 196612
  36.3 0.6 copy-start.8
  38.0 0.7 copy-start.10
  41.7 1.0 copy-start.5
  44.3 0.6 copy-start.18
  45.3 0.6 copy-start.12
  45.9 3.4 copy-start.3
  67.5 1.9 copy-start.4
  71.6 3.2 copy-start.17
  71.6 4.4 copy-start.9
  71.6 6.9 %copy-start.7 = (s32[256,64]{0,1:T(8,128)S(1)}, s32[256,64]{0,1:T(8,128)}, u32[]{:S(2)}) copy-start(s32[256,64]{0,1:T(8,128)} %param.15) | copy-start | bytes 196612
  71.6 6.9 %copy-start.11 = (s32[32,1]{1,0:T(8,128)S(1)}, s32[32,1]{1,0:T(8,128)}, u32[]{:S(2)}) copy-start(s32[32,1]{1,0:T(8,128)} %copy-done.10) | copy-start | bytes 388
  71.6 6.9 %copy-start.13 = (s32[32,256]{1,0:T(8,128)S(1)}, s32[32,256]{1,0:T(8,128)}, u32[]{:S(2)}) copy-start(s32[32,256]{1,0:T(8,128)} %copy-done.12) | copy-start | bytes 98308
  78.6 406.0 %all-reduce.4.cloned.1.call-start = ((), (), s32[]{:S(2)}) async-start(), calls=%async_computation | async-start | bytes 8388608 | tf_op jit(solution)/shard_map/cond/branch_0_fun/psum | solution.py:333
  85.7 3.4 copy-start.14
  315.8 13.0 %copy-start = (bf16[640,256,128]{2,1,0:T(8,128)(2,1)S(1)}, bf16[640,256,128]{2,1,0:T(8,128)(2,1)}, u32[]{:S(2)}) copy-start(bf16[640,256,128]{2,1,0:T(8,128)(2,1)} %pack_relay.3.refs_0_) | copy-start | bytes 125829120 | tf_op jit(solution)/shard_map/cond
Sparse Core Ops, SparseCore 0:
  84.9 399.6 all-reduce.3

commit v2 on v1

v2 whole, which is shorter than its diff:
```python
import functools

import jax
import jax.numpy as jnp
from jax import lax
from jax.experimental import pallas as pl
from jax.experimental.pallas import tpu as pltpu
from jax.sharding import PartitionSpec as P

F32 = jnp.float32
BF16 = jnp.bfloat16
ROW_CAP = 5
POOL_CHUNK = 16
HOT_CAP = 64
PLANES = 4
HOT_PART = 4
HOT_IN = PLANES * HOT_PART
MESH = pl.DeviceIdType.MESH
LEVELS = ((8, 58, 10), (8, 64, 10), (12, 80, 16))


def any_spec():
    return pl.BlockSpec(memory_space=pl.ANY)


def smem_spec():
    return pl.BlockSpec(memory_space=pltpu.SMEM)


def vmem_spec():
    return pl.BlockSpec(memory_space=pltpu.VMEM)


def pack_pool_kernel(cfg, counts, near_ids, cross_ids, hot_ids, perm, k_pool, v_pool, x_near, x_cross, x_hot,
                     raw, head_major, in_sem, out_sem):
    per_dev, n_half, pair_cap = cfg
    n_chunk = per_dev // POOL_CHUNK

    def chunk_copies(chunk, slot):
        rows = pl.ds(chunk * POOL_CHUNK, POOL_CHUNK)
        return (pltpu.make_async_copy(k_pool.at[rows], raw.at[slot, 0], in_sem.at[slot, 0]),
                pltpu.make_async_copy(v_pool.at[rows], raw.at[slot, 1], in_sem.at[slot, 1]))

    for copy in chunk_copies(0, 0):
        copy.start()

    def turn_chunk(chunk, carry):
        slot = lax.rem(chunk, 2)

        @pl.when(chunk + 1 < n_chunk)
        def _():
            for copy in chunk_copies(chunk + 1, 1 - slot):
                copy.start()

        for copy in chunk_copies(chunk, slot):
            copy.wait()
        for j in range(POOL_CHUNK):
            both = jnp.concatenate([raw[slot, 0, j], raw[slot, 1, j]], axis=1)
            turned = jnp.dot(perm[...], both, preferred_element_type=F32).astype(BF16)
            head_major[chunk * POOL_CHUNK + j, 0:128, :] = turned[:, 0:128]
            head_major[chunk * POOL_CHUNK + j, 128:256, :] = turned[:, 128:256]
        return carry

    lax.fori_loop(0, n_chunk, turn_chunk, 0)

    def start_list(ids, row, count, dest, base):
        def body(k, carry):
            pltpu.make_async_copy(head_major.at[ids[row, k]], dest.at[base + k], out_sem).start()
            return carry
        lax.fori_loop(0, count, body, 0)

    start_list(cross_ids, 0, counts[n_half], x_cross, 0)
    total = counts[n_half]
    for q in range(2):
        start_list(hot_ids, q, counts[n_half + 1 + q], x_hot, q * HOT_PART)
        total = total + counts[n_half + 1 + q]
    for q in range(n_half):
        start_list(near_ids, q, counts[q], x_near, q * pair_cap)
        total = total + counts[q]

    def drain(k, carry):
        pltpu.make_async_copy(head_major.at[0], x_near.at[0], out_sem).wait()
        return carry
    lax.fori_loop(0, total, drain, 0)


def pack_relay_kernel(cfg, counts, ids, arrived, x_out, stage, in_sem, out_sem):
    n_half, far_cap, n_arrived = cfg

    whole = pltpu.make_async_copy(arrived, stage, in_sem)
    whole.start()
    whole.wait()
    total = 0
    for q in range(n_half):
        def store(k, carry, q=q):
            pltpu.make_async_copy(stage.at[ids[q, k]], x_out.at[q * far_cap + k], out_sem).start()
            return carry
        lax.fori_loop(0, counts[q], store, 0)
        total = total + counts[q]

    def drain(k, carry):
        pltpu.make_async_copy(stage.at[0], x_out.at[0], out_sem).wait()
        return carry
    lax.fori_loop(0, total, drain, 0)


def xor_bits(index, bits):
    out = index
    bit = 1
    while bit <= bits:
        if bits & bit:
            out = out + bit - 2 * bit * lax.rem(index // bit, 2)
        bit *= 2
    return out


def exchange_kernel(cfg, *refs):
    n_half, slot_cap, pair_send, n_cross, base = cfg
    first = n_cross > 0
    if first:
        x_pair, x_cross, x_hot, recv, arrived, own, send_sem, recv_sem, own_sem = refs
    else:
        x_pair, _, recv, own, send_sem, recv_sem, own_sem = refs
    me = lax.axis_index('pool')
    in_half = lax.rem(me, n_half)
    half = me // n_half
    n_cols = 2 * n_half // PLANES
    plane, col = me // n_cols, lax.rem(me, n_cols)
    own_group = recv.at[pl.ds(base + in_half * slot_cap, pair_send)]
    sends = []
    for j in range(1, n_half):
        sends.append((half * n_half + xor_bits(in_half, j),
                      x_pair.at[pl.ds(xor_bits(in_half, j) * slot_cap, pair_send)], own_group))
    own_copies = [(x_pair.at[pl.ds(in_half * slot_cap, pair_send)], own.at[pl.ds(0, pair_send)], own_group)]
    if first:
        hot_here = arrived.at[pl.ds(plane * HOT_PART, HOT_PART)]
        hot_for = lambda p: x_hot.at[pl.ds(lax.rem(p, 2) * HOT_PART, HOT_PART)]
        for j in range(1, PLANES):
            to = xor_bits(plane, j)
            sends.append((to * n_cols + col, hot_for(to), hot_here))
        sends.append(((1 - half) * n_half + in_half, x_cross.at[pl.ds(0, n_cross)],
                      arrived.at[pl.ds(HOT_IN, n_cross)]))
        own_copies.append((hot_for(plane), own.at[pl.ds(pair_send, HOT_PART)], hot_here))

    barrier = pltpu.get_barrier_semaphore()
    for peer, _, _ in sends:
        pl.semaphore_signal(barrier, inc=1, device_id=(peer,), device_id_type=MESH)
    own_in = [pltpu.make_async_copy(src, mid, own_sem.at[0, i]) for i, (src, mid, _) in enumerate(own_copies)]
    for copy in own_in:
        copy.start()
    pl.semaphore_wait(barrier, len(sends))
    copies = []
    for i, (peer, src, dst) in reversed(list(enumerate(sends))):
        copies.append(pltpu.make_async_remote_copy(
            src_ref=src, dst_ref=dst, send_sem=send_sem.at[i], recv_sem=recv_sem.at[i],
            device_id=(peer,), device_id_type=MESH))
        copies[-1].start()
    for copy in own_in:
        copy.wait()
    own_out = [pltpu.make_async_copy(mid, dst, own_sem.at[1, i]) for i, (_, mid, dst) in enumerate(own_copies)]
    for copy in own_out:
        copy.start()
    for copy in own_out + copies:
        copy.wait()


def attend_kernel(cfg, pos, targets, q_ref, kn_ref, vn_ref, perm, recv, k_pool, v_pool, k_new, v_new,
                  out_ref, k_out, v_out, kv, heads_out, sem, pool_buf, new_buf, pool_in, pool_done, new_sem):
    n_pref, block_len, kv_heads, groups, chunk_len, head_dim, n_req, per_dev, n_new = cfg
    req = pl.program_id(0)
    slot = lax.rem(req, 2)
    exp_scale = float(head_dim ** -0.5 * 1.4426950408889634)
    piece = 2 * per_dev // n_req

    def fetch(which, into):
        def body(k, carry):
            pltpu.make_async_copy(recv.at[pos[which, k]], kv.at[into, k], sem.at[into]).start()
            return carry
        lax.fori_loop(0, n_pref, body, 0, unroll=8)

    def pool_copies(step, at):
        rows = pl.ds(step * piece, piece)
        pairs = ((k_pool, k_out), (v_pool, v_out))
        return ([pltpu.make_async_copy(src.at[rows], pool_buf.at[at, i], pool_in.at[at, i])
                 for i, (src, _) in enumerate(pairs)],
                [pltpu.make_async_copy(pool_buf.at[at, i], dst.at[rows], pool_done.at[at, i])
                 for i, (_, dst) in enumerate(pairs)])

    new_in = [pltpu.make_async_copy(src, new_buf.at[i], new_sem.at[i]) for i, src in enumerate((k_new, v_new))]

    def new_out(i, which):
        dst = (k_out, v_out)[which]
        return pltpu.make_async_copy(new_buf.at[which, i], dst.at[targets[i]], new_sem.at[2])

    @pl.when(req == 0)
    def _():
        fetch(0, 0)
        for copy in pool_copies(0, 0)[0] + new_in:
            copy.start()

    @pl.when(req + 1 < n_req)
    def _():
        fetch(req + 1, 1 - slot)

    n_step = n_req // 2
    for step in range(n_step):
        @pl.when(req == step)
        def _(step=step):
            at = step % 2
            ins, outs = pool_copies(step, at)
            for copy in ins:
                copy.wait()
            for copy in outs:
                copy.start()
            if step + 1 < n_step:
                if step > 0:
                    for copy in pool_copies(step - 1, 1 - at)[1]:
                        copy.wait()
                for copy in pool_copies(step + 1, 1 - at)[0]:
                    copy.start()

    @pl.when(req == n_step)
    def _():
        for step in (n_step - 2, n_step - 1):
            for copy in pool_copies(step, step % 2)[1]:
                copy.wait()
        for copy in new_in:
            copy.wait()
        for i in range(n_new):
            new_out(i, 0).start()
            new_out(i, 1).start()

    @pl.when(req == n_req - 1)
    def _():
        for i in range(n_new):
            new_out(i, 0).wait()
            new_out(i, 1).wait()

    pltpu.make_async_copy(recv.at[pl.ds(0, n_pref)], kv.at[slot], sem.at[slot]).wait()

    rows = chunk_len * groups
    token = lax.broadcasted_iota(jnp.int32, (rows, chunk_len), 0) // groups
    causal = lax.broadcasted_iota(jnp.int32, (rows, chunk_len), 1) <= token
    n_keys = n_pref * block_len
    nt = (((1,), (1,)), ((), ()))
    for h in range(kv_heads):
        q_h = q_ref[0, h]
        k_h = kv[slot, :, h * block_len:(h + 1) * block_len, :].reshape(n_keys, head_dim)
        v_at = (kv_heads + h) * block_len
        v_h = kv[slot, :, v_at:v_at + block_len, :].reshape(n_keys, head_dim)
        s_pref = lax.dot_general(q_h, k_h, nt, preferred_element_type=F32)
        s_self = lax.dot_general(q_h, kn_ref[0, h], nt, preferred_element_type=F32)
        s_self = jnp.where(causal, s_self, -jnp.inf)
        row_max = jnp.maximum(jnp.max(s_pref, axis=-1, keepdims=True), jnp.max(s_self, axis=-1, keepdims=True))
        e_pref = jnp.exp2((s_pref - row_max) * exp_scale)
        e_self = jnp.exp2((s_self - row_max) * exp_scale)
        total = jnp.sum(e_pref, axis=-1, keepdims=True) + jnp.sum(e_self, axis=-1, keepdims=True)
        inv = 1.0 / total
        p_pref = (e_pref * inv).astype(BF16)
        p_self = (e_self * inv).astype(BF16)
        acc = jnp.dot(p_pref, v_h, preferred_element_type=F32)
        acc = acc + jnp.dot(p_self, vn_ref[0, h], preferred_element_type=F32)
        heads_out[h] = acc.astype(BF16)
    span = 256 // kv_heads
    for g in range(rows // span):
        part = heads_out[:, g * span:(g + 1) * span, :].reshape(256, head_dim)
        out_ref[0, g * 256:(g + 1) * 256, :] = jnp.dot(perm[...], part, preferred_element_type=F32).astype(BF16)


def onehot(values, size):
    return (values[..., None] == jnp.arange(size, dtype=jnp.int32)).astype(BF16)


def ranks(ind):
    n = ind.shape[-1]
    strict = (jnp.arange(n)[:, None] < jnp.arange(n)[None, :]).astype(BF16)
    return jnp.einsum('...b,bk->...k', ind.astype(BF16), strict, preferred_element_type=F32).astype(jnp.int32)


def compact(ind, rank, value, size):
    hit = ind[..., :, None] & (rank[..., :, None] == jnp.arange(size))
    return jnp.sum(jnp.where(hit, value[..., :, None], 0), axis=-2)


def count(ind):
    return jnp.sum(ind.astype(jnp.int32), axis=-1)


def flat_ranks(ind):
    per_row = count(ind)
    before = jnp.cumsum(per_row, axis=-1) - per_row
    return ranks(ind) + before[..., None], jnp.sum(per_row, axis=-1)


def permutation(src_of_row):
    n = src_of_row.shape[0]
    return (src_of_row[:, None] == jnp.arange(n)[None, :]).astype(BF16)


def solution(mesh):
    n_dev = mesh.shape['pool']

    def local_step(queries, k_new, v_new, k_pool, v_pool, block_table, write_ids):
        req_count, chunk_len, q_heads, head_dim = queries.shape
        kv_heads = k_new.shape[2]
        groups = q_heads // kv_heads
        per_dev, block_len = k_pool.shape[0], k_pool.shape[1]
        n_pref = block_table.shape[1]
        block_rows = block_len * kv_heads
        pair_cap = req_count * ROW_CAP
        n_half = n_dev // 2
        n_cols = n_dev // PLANES
        far_cap = pair_cap + HOT_IN
        far_base = n_half * pair_cap
        n_recv = far_base + n_half * far_cap
        me = lax.axis_index('pool')
        half, partner = me // n_half, (me + n_half) % n_dev
        take = lambda x, at, axis: lax.dynamic_index_in_dim(x, at, axis, keepdims=False)

        table = block_table.reshape(n_dev, req_count * n_pref)
        want = jnp.einsum('deo,deb->dob', onehot(table // per_dev, n_dev), onehot(table % per_dev, per_dev),
                          preferred_element_type=F32) > 0
        popular = jnp.sum(want.astype(jnp.int32), axis=0)
        level_of = jnp.arange(2, n_dev + 2)
        at_least = jnp.sum((popular[None] >= level_of[:, None, None]).astype(jnp.int32), axis=(1, 2))
        threshold = 2 + jnp.sum((at_least > HOT_CAP).astype(jnp.int32))
        hot = popular >= threshold
        hot_rank = ranks(hot)
        hot = hot & (hot_rank < 2 * HOT_PART)
        hot_part = jnp.where(hot, hot_rank % 2, 2)
        rest = want & ~hot
        rank = ranks(rest)
        pair_count = count(rest)
        union = jnp.any(rest.reshape(2, n_half, n_dev, per_dev), axis=1)
        union_rank = ranks(union)
        union_count = count(union)
        other = (jnp.arange(2)[:, None] != jnp.arange(n_dev)[None, :] // n_half)
        hot_want = want[:, None] & (hot_part == jnp.arange(2)[:, None, None])[None]
        hot_num = count(hot_want).reshape(n_dev, 2, PLANES, n_cols)
        far_hot = jnp.sum(hot_num, axis=2).reshape(n_dev, n_half)
        dest_half = jnp.arange(n_dev) // n_half
        far_rest = jnp.where(dest_half[:, None] == 0, pair_count[:, n_half:], pair_count[:, :n_half])
        pair_max = jnp.max(pair_count)
        far_max = jnp.max(far_rest + far_hot)
        union_max = jnp.max(jnp.where(other, union_count, 0))

        ids = jnp.arange(per_dev, dtype=jnp.int32)
        halved = lambda x: lax.dynamic_slice_in_dim(x, half * n_half, n_half, 0)
        rest_half, rank_half, count_half = halved(rest), halved(rank), halved(pair_count)
        near_ids = compact(take(rest_half, me, 1), take(rank_half, me, 1), ids, pair_cap)
        cross_ids = compact(take(take(union, 1 - half, 0), me, 0), take(take(union_rank, 1 - half, 0), me, 0),
                            ids, per_dev)[None]
        part_mine = take(hot_part, me, 0) == jnp.arange(2)[:, None]
        hot_ids = compact(part_mine, take(hot_rank, me, 0)[None] // 2, ids, HOT_PART)
        counts = jnp.concatenate([take(count_half, me, 1), union_count[1 - half, me][None], count(part_mine)])

        plane, col = me // n_cols, me % n_cols
        by_col = lambda x: x.reshape(x.shape[:-2] + (PLANES, n_cols, per_dev))
        hot_col = take(take(by_col(halved(hot_want)), plane % 2, 1), col, 2)
        hot_at = jnp.arange(PLANES)[:, None] * HOT_PART + take(by_col(hot_rank), col, 1) // 2
        relay_want = jnp.concatenate([take(rest_half, partner, 1)[:, None], hot_col], axis=1)
        relay_at = jnp.concatenate([HOT_IN + take(take(union_rank, half, 0), partner, 0)[None], hot_at], axis=0)
        relay_rank, relay_counts = flat_ranks(relay_want)
        n_flat = (PLANES + 1) * per_dev
        relay_ids = compact(relay_want.reshape(n_half, n_flat), relay_rank.reshape(n_half, n_flat),
                            relay_at.reshape(1, n_flat), far_cap)

        my_table = lax.dynamic_slice_in_dim(block_table, me * req_count, req_count, 0)
        owner = jnp.arange(n_dev)
        group = (owner % n_half)[:, None]
        my_rank = take(rank, me, 0)
        is_near = (owner // n_half == half)[:, None]
        place = jnp.where(is_near, group * pair_cap + my_rank, far_base + group * far_cap + my_rank)
        my_hot = by_col(take(hot_want, me, 0)).transpose(0, 2, 1, 3)
        my_hot_rank = flat_ranks(my_hot)[0].transpose(0, 2, 1, 3).reshape(2, n_dev, per_dev)
        my_hot_rank = jnp.where(hot_part == 0, my_hot_rank[0], my_hot_rank[1])
        holder = jnp.where(hot_part == 1, n_cols, 0) + (owner % n_cols)[:, None]
        my_far_rest = take(far_rest, me, 0).reshape(2, 1, n_cols)
        before = jnp.broadcast_to(my_far_rest, (2, PLANES, n_cols)).reshape(2, n_dev, 1)
        before = jnp.where(hot_part == 1, before[1], before[0])
        place = jnp.where(hot, far_base + holder * far_cap + before + my_hot_rank, place)
        pos = place.reshape(-1)[my_table]

        block_shape = (2 * block_rows, head_dim)
        shaped = lambda n: jax.ShapeDtypeStruct((n,) + block_shape, BF16)
        row = jnp.arange(block_rows)
        turn = permutation((row % block_len) * kv_heads + row // block_len)
        flat_pool = (per_dev, block_rows, head_dim)
        k_flat, v_flat = k_pool.reshape(flat_pool), v_pool.reshape(flat_pool)
        x_near, x_cross, x_hot = pl.pallas_call(
            functools.partial(pack_pool_kernel, (per_dev, n_half, pair_cap)),
            out_shape=(shaped(n_half * pair_cap), shaped(per_dev), shaped(2 * HOT_PART)),
            in_specs=[smem_spec()] * 4 + [vmem_spec()] + [any_spec()] * 2,
            out_specs=(any_spec(),) * 3,
            scratch_shapes=[
                pltpu.VMEM((2, 2, POOL_CHUNK, block_rows, head_dim), BF16),
                pltpu.VMEM((per_dev,) + block_shape, BF16),
                pltpu.SemaphoreType.DMA((2, 2)),
                pltpu.SemaphoreType.DMA,
            ],
            compiler_params=pltpu.CompilerParams(vmem_limit_bytes=40 << 20),
            name='pack_pool',
        )(counts, near_ids, cross_ids, hot_ids, turn, k_flat, v_flat)

        rows = chunk_len * groups
        q_heads_major = queries.reshape(req_count, chunk_len, kv_heads, groups, head_dim)
        q_heads_major = q_heads_major.transpose(0, 2, 1, 3, 4).reshape(req_count, kv_heads, rows, head_dim)
        kn = k_new.transpose(0, 2, 1, 3)
        vn = v_new.transpose(0, 2, 1, 3)
        span_tok = 256 // q_heads
        out_row = jnp.arange(256)
        tok, head, grp = out_row // q_heads, (out_row % q_heads) // groups, out_row % groups
        back = permutation(head * (span_tok * groups) + tok * groups + grp)

        def exchange(level, near_send, n_cross, far_send, x_near, x_cross, x_hot, relay_counts, relay_ids):
            n_arrived = HOT_IN + n_cross

            def exchange_call(first, send, out_shape, n_in, alias, name):
                n_copy = n_half + PLANES
                return pl.pallas_call(
                    functools.partial(exchange_kernel, (
                        n_half, pair_cap if first else far_cap, send, n_cross if first else 0,
                        0 if first else far_base)),
                    out_shape=out_shape, in_specs=[any_spec()] * n_in,
                    out_specs=(any_spec(),) * 2 if first else any_spec(),
                    scratch_shapes=[
                        pltpu.VMEM((send + HOT_PART,) + block_shape, BF16), pltpu.SemaphoreType.DMA((n_copy,)),
                        pltpu.SemaphoreType.DMA((n_copy,)), pltpu.SemaphoreType.DMA((2, 2))],
                    input_output_aliases=alias,
                    compiler_params=pltpu.CompilerParams(
                        collective_id=2 * level + (0 if first else 1), has_side_effects=True,
                        vmem_limit_bytes=8 << 20),
                    name=name)

            recv, arrived = exchange_call(True, near_send, (shaped(n_recv), shaped(n_arrived)), 3, {},
                                          'exchange_near')(x_near, x_cross, x_hot)
            x_relay = pl.pallas_call(
                functools.partial(pack_relay_kernel, (n_half, far_cap, n_arrived)),
                out_shape=shaped(n_half * far_cap),
                in_specs=[smem_spec()] * 2 + [any_spec()], out_specs=any_spec(),
                scratch_shapes=[pltpu.VMEM((n_arrived,) + block_shape, BF16), pltpu.SemaphoreType.DMA,
                                pltpu.SemaphoreType.DMA],
                compiler_params=pltpu.CompilerParams(vmem_limit_bytes=24 << 20), name='pack_relay',
            )(relay_counts, relay_ids, arrived)
            return exchange_call(False, far_send, shaped(n_recv), 2, {1: 0}, 'exchange_far')(x_relay, recv)

        sizes = tuple(LEVELS) + ((pair_cap, per_dev, far_cap),)
        level = jnp.int32(0)
        for near_send, n_cross, far_send in LEVELS:
            over = (pair_max > near_send) | (union_max > n_cross) | (far_max > far_send)
            level = level + over.astype(jnp.int32)
        recv = lax.switch(level, [functools.partial(exchange, i, *s) for i, s in enumerate(sizes)],
                          x_near, x_cross, x_hot, relay_counts, relay_ids)

        cfg = (n_pref, block_len, kv_heads, groups, chunk_len, head_dim, req_count, per_dev, write_ids.size)
        new_shape = (write_ids.size, block_rows, head_dim)
        row_block = lambda *dims: pl.BlockSpec((1,) + dims, lambda r: (r,) + (0,) * len(dims))
        attn, k_pool_out, v_pool_out = pl.pallas_call(
            functools.partial(attend_kernel, cfg),
            out_shape=(jax.ShapeDtypeStruct((req_count, chunk_len * q_heads, head_dim), BF16),
                       jax.ShapeDtypeStruct(flat_pool, BF16), jax.ShapeDtypeStruct(flat_pool, BF16)),
            grid=(req_count,),
            in_specs=[
                smem_spec(), smem_spec(), row_block(kv_heads, rows, head_dim), row_block(kv_heads, chunk_len, head_dim),
                row_block(kv_heads, chunk_len, head_dim), pl.BlockSpec((256, 256), lambda r: (0, 0)),
            ] + [any_spec()] * 5,
            out_specs=(row_block(chunk_len * q_heads, head_dim), any_spec(), any_spec()),
            scratch_shapes=[
                pltpu.VMEM((2, n_pref) + block_shape, BF16),
                pltpu.VMEM((kv_heads, rows, head_dim), BF16),
                pltpu.SemaphoreType.DMA((2,)),
                pltpu.VMEM((2, 2, 2 * per_dev // req_count, block_rows, head_dim), BF16),
                pltpu.VMEM((2,) + new_shape, BF16),
                pltpu.SemaphoreType.DMA((2, 2)),
                pltpu.SemaphoreType.DMA((2, 2)),
                pltpu.SemaphoreType.DMA((3,)),
            ],
            compiler_params=pltpu.CompilerParams(
                vmem_limit_bytes=56 << 20, dimension_semantics=('arbitrary',)),
            name='attend',
        )(pos, write_ids.reshape(-1), q_heads_major, kn, vn, back, recv, k_flat, v_flat,
          k_new.reshape(new_shape), v_new.reshape(new_shape))
        attn_out = attn.reshape(req_count, chunk_len, q_heads, head_dim)
        return attn_out, k_pool_out.reshape(k_pool.shape), v_pool_out.reshape(v_pool.shape)

    row_spec = P('pool')
    return jax.shard_map(local_step, mesh=mesh, in_specs=(row_spec, row_spec, row_spec, row_spec, row_spec, P(), row_spec), out_specs=(row_spec, row_spec, row_spec), check_vma=False)
```

time: 536 us -> 470 us (0.88)
  local copies, waits for them, and re-layouts: 64.9 us -> 18.4 us
  waiting for transfers between devices: 33.7 us -> 0 us
  Pallas kernels: 405 us -> 423 us
  between operations: 17.4 us -> 6.49 us
    psum x1 -> x0, waiting for transfers between devices: 33.2 us -> none  [exchange_and_attend(): hot_all = lax.psum(x_hot, 'pool')]
    unnamed x35 -> x33, local copies, waits for them, and re-layouts: 30.2 us -> 6.19 us
    pallas_call x4, Pallas kernels: 387 us -> 405 us  [the longest x1 212 us: exchange(): exchange_call(True, near_send, (shaped(n_recv), shaped(n_arrived)), 3, {}...]
    cond x6 -> x0, local copies, waits for them, and re-layouts: 13.6 us -> none
    scatter x2 -> x0, local copies, waits for them, and re-layouts: 5.79 us -> none  [the longest x1 2.9 us: local_step(): k_pool_out = k_pool.at[targets].set(k_new.reshape(new_shape))]
  transfers between devices with their start and end apart: 1 -> 0, of which waited for: 1 -> 0; matrix products, arithmetic and copies ran while one was open for 2% -> 0% of each run, Pallas kernels for 64% -> 0%
where the time goes in v2:
time: 470 us; the launch traced here: 469 us
  Pallas kernels  423 us (90%)
  local copies, waits for them, and re-layouts  18.4 us (4%)
  other arithmetic  14.7 us (3%)
  between operations  6.49 us (1%)
  matrix products  6.07 us (1%)
    pallas_call x1, Pallas kernels, exchange(): exchange_call(True, near_send, (shaped(n_recv), shaped(n_arrived)), 3, {}...  212 us
    pallas_call x1, Pallas kernels, exchange(): exchange_call(False, far_send, shaped(n_recv), 2, {1: 0}, 'exchange_far')  145 us
    pallas_call x1, Pallas kernels, local_step(): pl.pallas_call(functools.partial(attend_kernel, cfg), out_shape=(jax.Shap...  43.1 us
    pallas_call x1, Pallas kernels, local_step(): pl.pallas_call(functools.partial(pack_pool_kernel, (per_dev, n_half, pair...  17.8 us

profile of v2, /device:TPU:0, one launch (start us, length us, event | category | flops | bytes accessed | tf_op | source)
XLA Modules:
  0.0 469.1 jit_solution(14346179322378878368)
XLA Ops:
  0.7 0.9 copy.52
  1.6 0.1 reshape.390
  1.7 0.1 add_select_fusion.1
  1.8 4.3 fusion.7
  6.1 0.1 convert_reduce_fusion.3
  6.3 0.7 convert_reduce_fusion.2
  7.0 1.2 fusion.49
  8.8 0.2 fusion.51
  9.0 0.4 convolution_convert_fusion
  9.4 0.9 copy-done.9
  10.4 0.2 broadcast_and_fusion.1
  10.7 0.4 select_reduce_fusion.1.near_ids
  11.0 0.6 convert_reduce_fusion.1
  11.6 0.2 dynamic-slice_reduce_fusion
  11.8 0.2 bitcast_reduce_fusion
  12.0 0.1 convert_reduce_fusion.6
  12.1 0.6 dynamic_slice.79
  12.8 0.1 convert_reduce_fusion.8
  12.9 0.7 pad_add_fusion.2.counts
  13.6 0.2 convolution_convert_fusion.2
  13.8 0.2 select_reduce_fusion.2
  14.0 0.1 select_reduce_fusion.3.hot_ids
  14.2 0.1 fusion.23.perm
  14.3 3.4 copy-done
  17.7 17.8 %pack_pool.1 = (bf16[640,256,128]{2,1,0:T(8,128)(2,1)}, bf16[256,256,128]{2,1,0:T(8,128)(2,1)}, bf16[8,256,128]{2,1,0:T(8,128)(2,1)S(1)}) custom-call(s32[19]{0:T(128)S(1)} %pad_add_fusion.2.counts, s32[16,40]{1,0:T(8,128)S(1)} %select_reduce_fusion.1.near_ids, s32[1,256]{1,0:T(1,128)S(1)} %bitcast.116, s32[2,4]{1,0:T(2,128)S(1)} %select_reduce_fusion.3.hot_ids, ...), custom_call_target="tpu_custom_call" | custom-call | tf_op jit(solution)/shard_map/pack_pool/pallas_call | solution.py:390
  35.5 0.2 and_convert_fusion
  35.7 0.3 broadcast_and_fusion
  36.1 0.8 copy-done.3
  36.8 0.1 dynamic-slice_bitcast_fusion
  37.0 0.1 constant_dynamic-slice_fusion.2
  37.1 0.2 convert_reduce_fusion.4
  37.3 0.2 fusion.9
  37.6 0.1 fusion.35
  37.7 1.2 select_reduce_fusion
  38.9 0.6 broadcast_compare_fusion.1
  39.5 1.2 convert_reduce_fusion
  40.7 0.1 copy.58
  40.8 0.1 copy.59
  40.8 1.4 add_reduce_fusion
  42.9 0.6 and_select_fusion.8
  43.5 0.7 fusion.42
  44.8 0.6 reduce_max.27
  48.6 362.6 %conditional.1 = (bf16[1536,256,128]{2,1,0:T(8,128)(2,1)}) conditional(s32[]{:T(128)} %clamp.53, (bf16[640,256,128]{2,1,0:T(8,128)(2,1)}, bf16[256,256,128]{2,1,0:T(8,128)(2,1)}, bf16[8,256,128]{2,1,0:T(8,128)(2,1)S(1)}, s32[16]{0:T(128)S(1)}, s32[16,56]{1,0:T(8,128)S(1)}) %tuple.20, ...), branch_computations={%region_21.22_spmd, %region_22.23_spmd, %region_23.24_spmd, %regio... | conditional | bytes 8 | solution.py:452
  48.6 212.3 %exchange_near.4 = (bf16[1536,256,128]{2,1,0:T(8,128)(2,1)}, bf16[74,256,128]{2,1,0:T(8,128)(2,1)S(1)}) custom-call(bf16[640,256,128]{2,1,0:T(8,128)(2,1)} %get-tuple-element.41.refs_0_, bf16[256,256,128]{2,1,0:T(8,128)(2,1)} %get-tuple-element.48.refs_1_, bf16[8,256,128]{2,1,0:T(8,128)(2,1)S(1)} %get-tuple-element.49.refs_2_), custom_call_target="tpu_custom_call" | custom-call | tf_op jit(solution)/shard_map/cond/branch_0_fun/exchange_near/pallas_call | solution.py:435
  260.9 5.1 %pack_relay.4.refs_0_ = bf16[896,256,128]{2,1,0:T(8,128)(2,1)} custom-call(s32[16]{0:T(128)S(1)} %get-tuple-element.24.counts, s32[16,56]{1,0:T(8,128)S(1)} %get-tuple-element.40.ids, bf16[74,256,128]{2,1,0:T(8,128)(2,1)S(1)} %get-tuple-element.50.arrived), custom_call_target="tpu_custom_call" | custom-call | tf_op jit(solution)/shard_map/cond/branch_0_fun/pack_relay/pallas_call | solution.py:437
  266.0 145.0 %exchange_far.4 = bf16[1536,256,128]{2,1,0:T(8,128)(2,1)} custom-call(bf16[896,256,128]{2,1,0:T(8,128)(2,1)} %pack_relay.4.refs_0_, bf16[1536,256,128]{2,1,0:T(8,128)(2,1)} %get-tuple-element.51.refs_1_), custom_call_target="tpu_custom_call", output_to_operand_aliasing={{}: (1, {})} | custom-call | tf_op jit(solution)/shard_map/cond/branch_0_fun/exchange_far/pallas_call | solution.py:445
  411.2 0.7 constant_dynamic-slice_fusion.9
  411.9 0.1 slice_bitcast_fusion.3
  412.0 0.1 broadcast_in_dim.101
  412.1 0.1 broadcast_in_dim.96
  412.2 0.9 convert_reduce_fusion.7
  413.2 0.9 fusion.11
  414.1 0.9 fusion.32
  415.0 0.1 compare_select_fusion
  415.1 0.1 copy.53
  415.2 0.1 reshape.410
  415.2 3.1 gather_fusion
  418.4 0.7 reshape.409.pos
  419.1 1.2 copy_bitcast_fusion
  420.3 4.1 copy.55
  424.4 0.7 fusion.20.perm
  425.1 0.1 copy.54
  425.2 0.6 reshape.393.targets
  425.8 43.1 %attend.1 = (bf16[8,1024,128]{2,1,0:T(8,128)(2,1)}, bf16[256,128,128]{2,1,0:T(8,128)(2,1)}, bf16[256,128,128]{2,1,0:T(8,128)(2,1)}) custom-call(s32[8,64]{1,0:T(8,128)} %reshape.409.pos, s32[16]{0:T(128)} %reshape.393.targets, bf16[8,8,128,128]{3,2,1,0:T(8,128)(2,1)} %bitcast.120, bf16[8,8,32,128]{3,2,1,0:T(8,128)(2,1)} %get-tuple-element.110.kn_ref, ...), custom_call_target="tpu_custom_call" | custom-call | tf_op jit(solution)/shard_map/attend/pallas_call | solution.py:458
  (59 shorter events, 0.5 us)
Async XLA Ops:
  9.0 26.5 %copy-start.7 = (pred[32,256]{1,0:T(8,128)(4,1)}, pred[32,256]{1,0:T(8,128)(4,1)S(1)}, u32[]{:S(2)}) copy-start(pred[32,256]{1,0:T(8,128)(4,1)S(1)} %get-tuple-element.93) | copy-start | bytes 24580
  9.0 28.5 %copy-start.4 = (s32[32,256]{1,0:T(8,128)}, s32[32,256]{1,0:T(8,128)S(1)}, u32[]{:S(2)}) copy-start(s32[32,256]{1,0:T(8,128)S(1)} %get-tuple-element.102) | copy-start | bytes 98308
  9.4 1.0 copy-start.9
  14.3 3.4 copy-start
  36.0 0.8 copy-start.3
  48.5 365.5 %copy-start.5 = (s32[32,256]{1,0:T(8,128)S(1)}, s32[32,256]{1,0:T(8,128)}, u32[]{:S(2)}) copy-start(s32[32,256]{1,0:T(8,128)} %copy-done.4) | copy-start | bytes 98308
  48.5 365.5 %copy-start.8 = (pred[32,256]{1,0:T(8,128)(4,1)S(1)}, pred[32,256]{1,0:T(8,128)(4,1)}, u32[]{:S(2)}) copy-start(pred[32,256]{1,0:T(8,128)(4,1)} %copy-done.7) | copy-start | bytes 24580
  48.6 365.5 %copy-start.11 = (s32[32]{0:T(128)S(1)}, s32[32]{0:T(128)}, u32[]{:S(2)}) copy-start(s32[32]{0:T(128)} %get-tuple-element.106) | copy-start | bytes 388
  48.6 365.5 %copy-start.12 = (pred[32]{0:T(512)(128)(4,1)S(1)}, pred[32]{0:T(512)(128)(4,1)}, u32[]{:S(2)}) copy-start(pred[32]{0:T(512)(128)(4,1)} %get-tuple-element.107) | copy-start | bytes 100
  48.6 365.5 %copy-start.13 = (s32[32]{0:T(128)S(1)}, s32[32]{0:T(128)}, u32[]{:S(2)}) copy-start(s32[32]{0:T(128)} %get-tuple-element.104) | copy-start | bytes 388
  48.6 366.4 %copy-start.6 = (s32[256,64]{0,1:T(8,128)S(1)}, s32[256,64]{0,1:T(8,128)}, u32[]{:S(2)}) copy-start(s32[256,64]{0,1:T(8,128)} %param.16) | copy-start | bytes 196612
  48.6 370.5 %copy-start.1 = (bf16[8,32,8,128]{3,2,1,0:T(8,128)(2,1)S(1)}, bf16[8,32,8,128]{3,2,1,0:T(8,128)(2,1)}, u32[]{:S(2)}) copy-start(bf16[8,32,8,128]{3,2,1,0:T(8,128)(2,1)} %param.13) | copy-start | bytes 1572868
  48.6 370.5 %copy-start.2 = (bf16[8,32,8,128]{3,2,1,0:T(8,128)(2,1)S(1)}, bf16[8,32,8,128]{3,2,1,0:T(8,128)(2,1)}, u32[]{:S(2)}) copy-start(bf16[8,32,8,128]{3,2,1,0:T(8,128)(2,1)} %param.12) | copy-start | bytes 1572868
  411.2 13.9 %copy-start.10 = (s32[8,2]{0,1:T(2,128)S(1)}, s32[8,2]{0,1:T(2,128)}, u32[]{:S(2)}) copy-start(s32[8,2]{0,1:T(2,128)} %param.17) | copy-start | bytes 196

commit v3 on v2

v3 whole, which is shorter than its diff:
```python
import functools

import jax
import jax.numpy as jnp
from jax import lax
from jax.experimental import pallas as pl
from jax.experimental.pallas import tpu as pltpu
from jax.sharding import PartitionSpec as P

F32 = jnp.float32
BF16 = jnp.bfloat16
ROW_CAP = 5
POOL_CHUNK = 16
HOT_CAP = 64
PLANES = 4
HOT_PART = 4
HOT_IN = PLANES * HOT_PART
NEAR_ROW, RELAY_ROW, CROSS_ROW, HOT_ROW, LEVEL_ROW, POS_ROW, PLAN_ROWS = 0, 16, 32, 33, 35, 36, 40
COUNT_LANE = 128
MESH = pl.DeviceIdType.MESH
ORDER = (14, 8, 4, 6, 12, 10, 2, 15, 9, 5, 7, 13, 11, 3, 1)
LEVELS = ((8, 58, 10), (8, 64, 10), (12, 80, 16))


def any_spec():
    return pl.BlockSpec(memory_space=pl.ANY)


def smem_spec():
    return pl.BlockSpec(memory_space=pltpu.SMEM)


def vmem_spec():
    return pl.BlockSpec(memory_space=pltpu.VMEM)


def dot_nn(a, b):
    return jnp.dot(a.astype(BF16), b.astype(BF16), preferred_element_type=F32)


def flag(cond):
    return jnp.where(cond, 1.0, 0.0)


def iota(shape, dim):
    return lax.broadcasted_iota(jnp.int32, shape, dim)


def permutation(n, src_of_row):
    return flag(src_of_row(iota((n, n), 0)) == iota((n, n), 1)).astype(BF16)


def plan_kernel(cfg, table, out, want_s, key_s, hot_s, count_s, union_s):
    n_dev, n_half, per_dev, pair_cap, far_cap, far_base, levels = cfg
    n_cols = n_dev // PLANES
    n_entry = table.shape[1]
    me = lax.axis_index('pool')
    half, in_half = me // n_half, lax.rem(me, n_half)
    partner = (1 - half) * n_half + in_half
    plane, col = me // n_cols, lax.rem(me, n_cols)
    tri = flag(iota((per_dev, per_dev), 0) < iota((per_dev, per_dev), 1)).astype(BF16)
    rowsum = lambda x: jnp.sum(x, axis=1, keepdims=True)

    def hot_entries(dest):
        row = table[pl.ds(dest, 1), :]
        owner = row // per_dev
        return (flag(iota((n_dev, n_entry), 0) == owner).astype(BF16),
                flag(iota((per_dev, n_entry), 0) == row - owner * per_dev).astype(BF16))

    def find(dest, popular):
        by_owner, by_block = hot_entries(dest)
        hits = lax.dot_general(by_owner, by_block, (((1,), (1,)), ((), ())), preferred_element_type=F32)
        want = flag(hits > 0)
        want_s[dest] = want
        return popular + want
    popular = lax.fori_loop(0, n_dev, find, jnp.zeros((n_dev, per_dev), F32))

    def search(_, bounds):
        low, high = bounds
        mid = (low + high) // 2
        fits = jnp.sum(flag(popular >= mid.astype(F32))) <= HOT_CAP
        return jnp.where(fits, low, mid + 1), jnp.where(fits, mid, high)
    steps = n_dev.bit_length()
    threshold, _ = lax.fori_loop(0, steps, search, (jnp.int32(2), jnp.int32(n_dev + 1)))
    hot = flag(popular >= threshold.astype(F32))
    hot_rank = dot_nn(hot, tri)
    hot = hot * flag(hot_rank < 2 * HOT_PART)
    hot_half = jnp.floor(hot_rank * 0.5)
    hot_part = hot_rank - 2 * hot_half
    hot_of = [hot * flag(hot_part == p) for p in range(2)]
    for p in range(2):
        hot_s[p] = hot_of[p]
    hot_s[2] = hot_half

    def rank_rest(dest, carry):
        union, pair_max, far_max = carry
        want = want_s[dest]
        rest = want * (1 - hot)
        key_s[dest] = jnp.where(rest > 0, dot_nn(rest, tri), -1.0)
        num = rowsum(rest)
        count_s[dest] = jnp.broadcast_to(num, (n_dev, 128))
        held = []
        for p in range(2):
            per_owner = rowsum(want * hot_of[p])
            held.append(sum(per_owner[q * n_cols:(q + 1) * n_cols] for q in range(PLANES)))
        across = jnp.where(dest < n_half, num[n_half:], num[:n_half])
        far = across + jnp.concatenate(held, axis=0)
        return jnp.maximum(union, rest), jnp.maximum(pair_max, num), jnp.maximum(far_max, far)

    def rank_half(first, maxima):
        zero = jnp.zeros((n_dev, per_dev), F32)
        return lax.fori_loop(first, first + n_half, rank_rest, (zero,) + maxima)
    union0, pair_max, far_max = rank_half(0, (jnp.zeros((n_dev, 1), F32), jnp.zeros((n_half, 1), F32)))
    union1, pair_max, far_max = rank_half(n_half, (pair_max, far_max))
    for h, union in enumerate((union0, union1)):
        union_s[h] = jnp.where(union > 0, dot_nn(union, tri), -1.0)
    union_max = jnp.maximum(jnp.max(rowsum(union0)[n_half:]), jnp.max(rowsum(union1)[:n_half]))
    pair_max, far_max = jnp.max(pair_max), jnp.max(far_max)
    level = jnp.int32(0)
    for near_send, n_cross, far_send in levels:
        over = (pair_max > near_send) | (union_max > n_cross) | (far_max > far_send)
        level = level + over.astype(jnp.int32)
    out[LEVEL_ROW:LEVEL_ROW + 1, :] = jnp.full((1, per_dev), level, jnp.int32)

    def compact(keys, values, size):
        place = iota((per_dev, size), 1).astype(F32)
        total = 0
        for key, value in zip(keys, values):
            total = total + jnp.sum(jnp.where(key == place, value, 0.0), axis=0, keepdims=True)
        return total

    def put(row, ids, num):
        out[row:row + 1, 0:ids.shape[1]] = ids.astype(jnp.int32)
        if ids.shape[1] < per_dev:
            out[row:row + 1, COUNT_LANE:] = jnp.broadcast_to(num, (1, per_dev - COUNT_LANE)).astype(jnp.int32)

    ids = iota((per_dev, 1), 0).astype(F32)
    dests = [half * n_half + d for d in range(n_half)]
    stack = lambda ref, at: jnp.concatenate([ref[d, pl.ds(at, 1), :] for d in dests], axis=0)
    near_keys = stack(key_s, me)
    relay_keys = [stack(key_s, partner)]
    relay_num = [rowsum(flag(relay_keys[0] >= 0))]
    mine = lax.rem(plane, 2)
    for q in range(PLANES):
        here = stack(want_s, q * n_cols + col) * hot_s[mine, pl.ds(q * n_cols + col, 1), :]
        before = sum(relay_num)
        relay_keys.append(jnp.where(here > 0, dot_nn(here, tri) + before, -1.0))
        relay_num.append(rowsum(here))
    relay_at = [HOT_IN + union_s[half, pl.ds(partner, 1), :]]
    for q in range(PLANES):
        relay_at.append(q * HOT_PART + hot_s[2, pl.ds(q * n_cols + col, 1), :])
    cross_key = union_s[1 - half, pl.ds(me, 1), :]
    hot_keys = [jnp.where(hot_s[p, pl.ds(me, 1), :] > 0, hot_s[2, pl.ds(me, 1), :], -1.0) for p in range(2)]
    rows = [near_keys] + relay_keys + relay_at + [cross_key] + hot_keys
    used = sum(r.shape[0] for r in rows)
    turned = jnp.concatenate(rows + [jnp.zeros((128 - used, per_dev), F32)], axis=0).T
    column = lambda i: turned[:, i:i + 1]
    at0 = n_half * (PLANES + 2)
    values = [column(at0 + q) for q in range(PLANES + 1)]
    near_num = rowsum(flag(near_keys >= 0))
    for d in range(n_half):
        put(NEAR_ROW + d, compact([column(d)], [ids], 128), near_num[d:d + 1])
        keys = [column(n_half * (q + 1) + d) for q in range(PLANES + 1)]
        put(RELAY_ROW + d, compact(keys, values, 128), sum(relay_num)[d:d + 1])
    last = at0 + PLANES + 1
    put(CROSS_ROW, compact([column(last)], [ids], per_dev), None)
    for p in range(2):
        put(HOT_ROW + p, compact([column(last + 1 + p)], [ids], 128), rowsum(flag(hot_keys[p] >= 0)))
    cross_num = rowsum(flag(cross_key >= 0)).astype(jnp.int32)
    out[LEVEL_ROW:LEVEL_ROW + 1, COUNT_LANE:] = jnp.broadcast_to(cross_num, (1, per_dev - COUNT_LANE))

    owner = iota((n_dev, 1), 0)
    group = lax.rem(owner, n_half).astype(F32)
    is_near = owner // n_half == half
    rest_at = jnp.where(is_near, group * pair_cap, far_base + group * far_cap) + key_s[me]
    num = count_s[me, :, 0:1]
    across = jnp.where(half == 0, num[n_half:], num[:n_half])
    place = rest_at
    for p in range(2):
        here = want_s[me] * hot_of[p]
        per_owner = rowsum(here)
        parts = [per_owner[q * n_cols:(q + 1) * n_cols] for q in range(PLANES)]
        holder = p * n_cols + iota((n_cols, 1), 0)
        start = far_base + holder.astype(F32) * far_cap + across[p * n_cols:(p + 1) * n_cols]
        starts = [start]
        for part in parts[:-1]:
            starts.append(starts[-1] + part)
        place = jnp.where(here > 0, jnp.concatenate(starts, axis=0) + dot_nn(here, tri), place)
    place = jnp.maximum(place, 0.0)
    high = jnp.floor(place * (1.0 / 256))
    by_owner, by_block = hot_entries(me)
    picked = dot_nn(high, by_block) * 256 + dot_nn(place - high * 256, by_block)
    pos = jnp.sum(picked * by_owner.astype(F32), axis=0, keepdims=True).astype(jnp.int32)
    for i in range(n_entry // per_dev):
        out[POS_ROW + i:POS_ROW + i + 1, :] = pos[:, i * per_dev:(i + 1) * per_dev]


def pack_pool_kernel(cfg, plan, k_pool, v_pool, x_near, x_cross, x_hot, raw, head_major, in_sem, out_sem):
    per_dev, n_half, pair_cap, block_len, kv_heads = cfg
    n_chunk = per_dev // POOL_CHUNK
    perm = permutation(block_len * kv_heads, lambda r: lax.rem(r, block_len) * kv_heads + r // block_len)

    def chunk_copies(chunk, slot):
        rows = pl.ds(chunk * POOL_CHUNK, POOL_CHUNK)
        return (pltpu.make_async_copy(k_pool.at[rows], raw.at[slot, 0], in_sem.at[slot, 0]),
                pltpu.make_async_copy(v_pool.at[rows], raw.at[slot, 1], in_sem.at[slot, 1]))

    for copy in chunk_copies(0, 0):
        copy.start()

    def turn_chunk(chunk, carry):
        slot = lax.rem(chunk, 2)

        @pl.when(chunk + 1 < n_chunk)
        def _():
            for copy in chunk_copies(chunk + 1, 1 - slot):
                copy.start()

        for copy in chunk_copies(chunk, slot):
            copy.wait()
        for j in range(POOL_CHUNK):
            both = jnp.concatenate([raw[slot, 0, j], raw[slot, 1, j]], axis=1)
            turned = jnp.dot(perm, both, preferred_element_type=F32).astype(BF16)
            head_major[chunk * POOL_CHUNK + j, 0:128, :] = turned[:, 0:128]
            head_major[chunk * POOL_CHUNK + j, 128:256, :] = turned[:, 128:256]
        return carry

    lax.fori_loop(0, n_chunk, turn_chunk, 0)

    def start_list(row, count, dest, base):
        def body(k, carry):
            pltpu.make_async_copy(head_major.at[plan[row, k]], dest.at[base + k], out_sem).start()
            return carry
        lax.fori_loop(0, count, body, 0)

    total = plan[LEVEL_ROW, COUNT_LANE]
    start_list(CROSS_ROW, total, x_cross, 0)
    for q in range(2):
        num = plan[HOT_ROW + q, COUNT_LANE]
        start_list(HOT_ROW + q, num, x_hot, q * HOT_PART)
        total = total + num
    for q in range(n_half):
        num = plan[NEAR_ROW + q, COUNT_LANE]
        start_list(NEAR_ROW + q, num, x_near, q * pair_cap)
        total = total + num

    def drain(k, carry):
        pltpu.make_async_copy(head_major.at[0], x_near.at[0], out_sem).wait()
        return carry
    lax.fori_loop(0, total, drain, 0)


def pack_relay_kernel(cfg, plan, arrived, x_out, stage, in_sem, out_sem):
    n_half, far_cap, n_arrived = cfg

    whole = pltpu.make_async_copy(arrived, stage, in_sem)
    whole.start()
    whole.wait()
    total = 0
    for q in range(n_half):
        def store(k, carry, q=q):
            pltpu.make_async_copy(stage.at[plan[RELAY_ROW + q, k]], x_out.at[q * far_cap + k], out_sem).start()
            return carry
        num = plan[RELAY_ROW + q, COUNT_LANE]
        lax.fori_loop(0, num, store, 0)
        total = total + num

    def drain(k, carry):
        pltpu.make_async_copy(stage.at[0], x_out.at[0], out_sem).wait()
        return carry
    lax.fori_loop(0, total, drain, 0)


def xor_bits(index, bits):
    out = index
    bit = 1
    while bit <= bits:
        if bits & bit:
            out = out + bit - 2 * bit * lax.rem(index // bit, 2)
        bit *= 2
    return out


def exchange_kernel(cfg, *refs):
    n_half, slot_cap, pair_send, n_cross, base = cfg
    first = n_cross > 0
    if first:
        x_pair, x_cross, x_hot, recv, arrived, own, send_sem, recv_sem, own_sem = refs
    else:
        x_pair, _, recv, own, send_sem, recv_sem, own_sem = refs
    me = lax.axis_index('pool')
    in_half = lax.rem(me, n_half)
    half = me // n_half
    n_cols = 2 * n_half // PLANES
    plane, col = me // n_cols, lax.rem(me, n_cols)
    own_group = recv.at[pl.ds(base + in_half * slot_cap, pair_send)]
    sends = []
    for j in ORDER:
        sends.append((half * n_half + xor_bits(in_half, j),
                      x_pair.at[pl.ds(xor_bits(in_half, j) * slot_cap, pair_send)], own_group))
    own_copies = [(x_pair.at[pl.ds(in_half * slot_cap, pair_send)], own.at[pl.ds(0, pair_send)], own_group)]
    if first:
        hot_here = arrived.at[pl.ds(plane * HOT_PART, HOT_PART)]
        hot_for = lambda p: x_hot.at[pl.ds(lax.rem(p, 2) * HOT_PART, HOT_PART)]
        sends.append(((1 - half) * n_half + in_half, x_cross.at[pl.ds(0, n_cross)],
                      arrived.at[pl.ds(HOT_IN, n_cross)]))
        for j in range(1, PLANES):
            to = xor_bits(plane, j)
            sends.append((to * n_cols + col, hot_for(to), hot_here))
        own_copies.append((hot_for(plane), own.at[pl.ds(pair_send, HOT_PART)], hot_here))

    barrier = pltpu.get_barrier_semaphore()
    for peer, _, _ in sends:
        pl.semaphore_signal(barrier, inc=1, device_id=(peer,), device_id_type=MESH)
    own_in = [pltpu.make_async_copy(src, mid, own_sem.at[0, i]) for i, (src, mid, _) in enumerate(own_copies)]
    for copy in own_in:
        copy.start()
    pl.semaphore_wait(barrier, len(sends))
    copies = []
    for i, (peer, src, dst) in enumerate(sends):
        copies.append(pltpu.make_async_remote_copy(
            src_ref=src, dst_ref=dst, send_sem=send_sem.at[i], recv_sem=recv_sem.at[i],
            device_id=(peer,), device_id_type=MESH))
        copies[-1].start()
    for copy in own_in:
        copy.wait()
    own_out = [pltpu.make_async_copy(mid, dst, own_sem.at[1, i]) for i, (_, mid, dst) in enumerate(own_copies)]
    for copy in own_out:
        copy.start()
    for copy in own_out + copies:
        copy.wait()


def attend_kernel(cfg, plan, targets, q_ref, kn_ref, vn_ref, recv, k_pool, v_pool, k_new, v_new,
                  out_ref, k_out, v_out, kv, q_heads, heads_out, sem, pool_buf, new_buf, pool_in, pool_done, new_sem):
    n_pref, block_len, kv_heads, groups, chunk_len, head_dim, n_req, per_dev, n_new = cfg
    req = pl.program_id(0)
    slot = lax.rem(req, 2)
    exp_scale = float(head_dim ** -0.5 * 1.4426950408889634)
    piece = 2 * per_dev // n_req
    per_row = per_dev // n_pref

    def fetch(which, into):
        def body(k, carry):
            pltpu.make_async_copy(recv.at[plan[POS_ROW + which // per_row, lax.rem(which, per_row) * n_pref + k]], kv.at[into, k], sem.at[into]).start()
            return carry
        lax.fori_loop(0, n_pref, body, 0, unroll=8)

    def pool_copies(step, at):
        rows = pl.ds(step * piece, piece)
        pairs = ((k_pool, k_out), (v_pool, v_out))
        return ([pltpu.make_async_copy(src.at[rows], pool_buf.at[at, i], pool_in.at[at, i])
                 for i, (src, _) in enumerate(pairs)],
                [pltpu.make_async_copy(pool_buf.at[at, i], dst.at[rows], pool_done.at[at, i])
                 for i, (_, dst) in enumerate(pairs)])

    new_in = [pltpu.make_async_copy(src, new_buf.at[i], new_sem.at[i]) for i, src in enumerate((k_new, v_new))]

    def new_out(i, which):
        dst = (k_out, v_out)[which]
        return pltpu.make_async_copy(new_buf.at[which, i], dst.at[targets[i]], new_sem.at[2])

    @pl.when(req == 0)
    def _():
        fetch(0, 0)
        for copy in pool_copies(0, 0)[0] + new_in:
            copy.start()

    @pl.when(req + 1 < n_req)
    def _():
        fetch(req + 1, 1 - slot)

    n_step = n_req // 2
    for step in range(n_step):
        @pl.when(req == step)
        def _(step=step):
            at = step % 2
            ins, outs = pool_copies(step, at)
            for copy in ins:
                copy.wait()
            for copy in outs:
                copy.start()
            if step + 1 < n_step:
                if step > 0:
                    for copy in pool_copies(step - 1, 1 - at)[1]:
                        copy.wait()
                for copy in pool_copies(step + 1, 1 - at)[0]:
                    copy.start()

    @pl.when(req == n_step)
    def _():
        for step in (n_step - 2, n_step - 1):
            for copy in pool_copies(step, step % 2)[1]:
                copy.wait()
        for copy in new_in:
            copy.wait()
        for i in range(n_new):
            new_out(i, 0).start()
            new_out(i, 1).start()

    @pl.when(req == n_req - 1)
    def _():
        for i in range(n_new):
            new_out(i, 0).wait()
            new_out(i, 1).wait()

    pltpu.make_async_copy(recv.at[pl.ds(0, n_pref)], kv.at[slot], sem.at[slot]).wait()

    rows = chunk_len * groups
    token = lax.broadcasted_iota(jnp.int32, (rows, chunk_len), 0) // groups
    causal = lax.broadcasted_iota(jnp.int32, (rows, chunk_len), 1) <= token
    n_keys = n_pref * block_len
    nt = (((1,), (1,)), ((), ()))
    span = 256 // kv_heads
    span_tok = span // groups
    to_heads = permutation(256, lambda r: lax.rem(r // groups, span_tok) * (kv_heads * groups)
                           + r // span * groups + lax.rem(r, groups))
    to_tokens = permutation(256, lambda r: lax.rem(r // groups, kv_heads) * span
                            + r // (kv_heads * groups) * groups + lax.rem(r, groups))
    new_heads = permutation(256, lambda r: lax.rem(r, chunk_len) * kv_heads + r // chunk_len)
    for g in range(rows // span):
        part = jnp.dot(to_heads, q_ref[0, g * 256:(g + 1) * 256, :], preferred_element_type=F32).astype(BF16)
        for h in range(kv_heads):
            q_heads[h, g * span:(g + 1) * span, :] = part[h * span:(h + 1) * span]
    new_kv = jnp.concatenate([kn_ref[0], vn_ref[0]], axis=1)
    new_kv = jnp.dot(new_heads, new_kv, preferred_element_type=F32).astype(BF16)
    for h in range(kv_heads):
        q_h = q_heads[h]
        k_own = new_kv[h * chunk_len:(h + 1) * chunk_len, 0:head_dim]
        v_own = new_kv[h * chunk_len:(h + 1) * chunk_len, head_dim:]
        k_h = kv[slot, :, h * block_len:(h + 1) * block_len, :].reshape(n_keys, head_dim)
        v_at = (kv_heads + h) * block_len
        v_h = kv[slot, :, v_at:v_at + block_len, :].reshape(n_keys, head_dim)
        s_pref = lax.dot_general(q_h, k_h, nt, preferred_element_type=F32)
        s_self = lax.dot_general(q_h, k_own, nt, preferred_element_type=F32)
        s_self = jnp.where(causal, s_self, -jnp.inf)
        row_max = jnp.maximum(jnp.max(s_pref, axis=-1, keepdims=True), jnp.max(s_self, axis=-1, keepdims=True))
        e_pref = jnp.exp2((s_pref - row_max) * exp_scale)
        e_self = jnp.exp2((s_self - row_max) * exp_scale)
        total = jnp.sum(e_pref, axis=-1, keepdims=True) + jnp.sum(e_self, axis=-1, keepdims=True)
        inv = 1.0 / total
        p_pref = (e_pref * inv).astype(BF16)
        p_self = (e_self * inv).astype(BF16)
        acc = jnp.dot(p_pref, v_h, preferred_element_type=F32)
        acc = acc + jnp.dot(p_self, v_own, preferred_element_type=F32)
        heads_out[h] = acc.astype(BF16)
    for g in range(rows // span):
        part = heads_out[:, g * span:(g + 1) * span, :].reshape(256, head_dim)
        out_ref[0, g * 256:(g + 1) * 256, :] = jnp.dot(to_tokens, part, preferred_element_type=F32).astype(BF16)


def solution(mesh):
    n_dev = mesh.shape['pool']

    def local_step(queries, k_new, v_new, k_pool, v_pool, block_table, write_ids):
        req_count, chunk_len, q_heads, head_dim = queries.shape
        kv_heads = k_new.shape[2]
        groups = q_heads // kv_heads
        per_dev, block_len = k_pool.shape[0], k_pool.shape[1]
        n_pref = block_table.shape[1]
        block_rows = block_len * kv_heads
        pair_cap = req_count * ROW_CAP
        n_half = n_dev // 2
        n_cols = n_dev // PLANES
        far_cap = pair_cap + HOT_IN
        far_base = n_half * pair_cap
        n_recv = far_base + n_half * far_cap
        plan = pl.pallas_call(
            functools.partial(plan_kernel, (n_dev, n_half, per_dev, pair_cap, far_cap, far_base, LEVELS)),
            out_shape=jax.ShapeDtypeStruct((PLAN_ROWS, per_dev), jnp.int32),
            in_specs=[vmem_spec()], out_specs=vmem_spec(),
            scratch_shapes=[
                pltpu.VMEM((n_dev, n_dev, per_dev), F32),
                pltpu.VMEM((n_dev, n_dev, per_dev), F32),
                pltpu.VMEM((3, n_dev, per_dev), F32),
                pltpu.VMEM((n_dev, n_dev, 128), F32),
                pltpu.VMEM((2, n_dev, per_dev), F32),
            ],
            compiler_params=pltpu.CompilerParams(vmem_limit_bytes=24 << 20),
            name='plan',
        )(block_table.reshape(n_dev, req_count * n_pref))

        block_shape = (2 * block_rows, head_dim)
        shaped = lambda n: jax.ShapeDtypeStruct((n,) + block_shape, BF16)
        flat_pool = (per_dev, block_rows, head_dim)
        k_flat, v_flat = k_pool.reshape(flat_pool), v_pool.reshape(flat_pool)
        x_near, x_cross, x_hot = pl.pallas_call(
            functools.partial(pack_pool_kernel, (per_dev, n_half, pair_cap, block_len, kv_heads)),
            out_shape=(shaped(n_half * pair_cap), shaped(per_dev), shaped(2 * HOT_PART)),
            in_specs=[smem_spec()] + [any_spec()] * 2,
            out_specs=(any_spec(),) * 3,
            scratch_shapes=[
                pltpu.VMEM((2, 2, POOL_CHUNK, block_rows, head_dim), BF16),
                pltpu.VMEM((per_dev,) + block_shape, BF16),
                pltpu.SemaphoreType.DMA((2, 2)),
                pltpu.SemaphoreType.DMA,
            ],
            compiler_params=pltpu.CompilerParams(vmem_limit_bytes=40 << 20),
            name='pack_pool',
        )(plan, k_flat, v_flat)

        rows = chunk_len * groups
        def exchange(level, near_send, n_cross, far_send, x_near, x_cross, x_hot, plan):
            n_arrived = HOT_IN + n_cross

            def exchange_call(first, send, out_shape, n_in, alias, name):
                n_copy = n_half + PLANES
                return pl.pallas_call(
                    functools.partial(exchange_kernel, (
                        n_half, pair_cap if first else far_cap, send, n_cross if first else 0,
                        0 if first else far_base)),
                    out_shape=out_shape, in_specs=[any_spec()] * n_in,
                    out_specs=(any_spec(),) * 2 if first else any_spec(),
                    scratch_shapes=[
                        pltpu.VMEM((send + HOT_PART,) + block_shape, BF16), pltpu.SemaphoreType.DMA((n_copy,)),
                        pltpu.SemaphoreType.DMA((n_copy,)), pltpu.SemaphoreType.DMA((2, 2))],
                    input_output_aliases=alias,
                    compiler_params=pltpu.CompilerParams(
                        collective_id=2 * level + (0 if first else 1), has_side_effects=True,
                        vmem_limit_bytes=8 << 20),
                    name=name)

            recv, arrived = exchange_call(True, near_send, (shaped(n_recv), shaped(n_arrived)), 3, {},
                                          'exchange_near')(x_near, x_cross, x_hot)
            x_relay = pl.pallas_call(
                functools.partial(pack_relay_kernel, (n_half, far_cap, n_arrived)),
                out_shape=shaped(n_half * far_cap),
                in_specs=[smem_spec(), any_spec()], out_specs=any_spec(),
                scratch_shapes=[pltpu.VMEM((n_arrived,) + block_shape, BF16), pltpu.SemaphoreType.DMA,
                                pltpu.SemaphoreType.DMA],
                compiler_params=pltpu.CompilerParams(vmem_limit_bytes=24 << 20), name='pack_relay',
            )(plan, arrived)
            return exchange_call(False, far_send, shaped(n_recv), 2, {1: 0}, 'exchange_far')(x_relay, recv)

        sizes = tuple(LEVELS) + ((pair_cap, per_dev, far_cap),)
        recv = lax.switch(plan[LEVEL_ROW, 0], [functools.partial(exchange, i, *s) for i, s in enumerate(sizes)],
                          x_near, x_cross, x_hot, plan)

        cfg = (n_pref, block_len, kv_heads, groups, chunk_len, head_dim, req_count, per_dev, write_ids.size)
        new_shape = (write_ids.size, block_rows, head_dim)
        row_block = lambda *dims: pl.BlockSpec((1,) + dims, lambda r: (r,) + (0,) * len(dims))
        attn, k_pool_out, v_pool_out = pl.pallas_call(
            functools.partial(attend_kernel, cfg),
            out_shape=(jax.ShapeDtypeStruct((req_count, chunk_len * q_heads, head_dim), BF16),
                       jax.ShapeDtypeStruct(flat_pool, BF16), jax.ShapeDtypeStruct(flat_pool, BF16)),
            grid=(req_count,),
            in_specs=[
                smem_spec(), smem_spec(), row_block(chunk_len * q_heads, head_dim),
                row_block(chunk_len * kv_heads, head_dim), row_block(chunk_len * kv_heads, head_dim),
            ] + [any_spec()] * 5,
            out_specs=(row_block(chunk_len * q_heads, head_dim), any_spec(), any_spec()),
            scratch_shapes=[
                pltpu.VMEM((2, n_pref) + block_shape, BF16),
                pltpu.VMEM((kv_heads, rows, head_dim), BF16),
                pltpu.VMEM((kv_heads, rows, head_dim), BF16),
                pltpu.SemaphoreType.DMA((2,)),
                pltpu.VMEM((2, 2, 2 * per_dev // req_count, block_rows, head_dim), BF16),
                pltpu.VMEM((2,) + new_shape, BF16),
                pltpu.SemaphoreType.DMA((2, 2)),
                pltpu.SemaphoreType.DMA((2, 2)),
                pltpu.SemaphoreType.DMA((3,)),
            ],
            compiler_params=pltpu.CompilerParams(
                vmem_limit_bytes=56 << 20, dimension_semantics=('arbitrary',)),
            name='attend',
        )(plan, write_ids.reshape(-1), queries.reshape(req_count, chunk_len * q_heads, head_dim),
          k_new.reshape(req_count, chunk_len * kv_heads, head_dim),
          v_new.reshape(req_count, chunk_len * kv_heads, head_dim), recv, k_flat, v_flat,
          k_new.reshape(new_shape), v_new.reshape(new_shape))
        attn_out = attn.reshape(req_count, chunk_len, q_heads, head_dim)
        return attn_out, k_pool_out.reshape(k_pool.shape), v_pool_out.reshape(v_pool.shape)

    row_spec = P('pool')
    return jax.shard_map(local_step, mesh=mesh, in_specs=(row_spec, row_spec, row_spec, row_spec, row_spec, P(), row_spec), out_specs=(row_spec, row_spec, row_spec), check_vma=False)
```

time: 470 us -> 410 us (0.87)
  Pallas kernels: 423 us -> 401 us
  other arithmetic: 14.7 us -> 0 us
  local copies, waits for them, and re-layouts: 18.4 us -> 5.63 us
  matrix products: 6.07 us -> 0 us
  between operations: 6.49 us -> 1.5 us
    pallas_call x1, Pallas kernels: 145 us -> 117 us  [exchange(): exchange_call(False, far_send, shaped(n_recv), 2, {1: 0}, 'exchange_far')]
    pallas_call x0 -> x1, Pallas kernels: none -> 16.5 us  [local_step(): pl.pallas_call(functools.partial(plan_kernel, (n_dev, n_half, per_dev, pa...]
    pallas_call x1, Pallas kernels: 212 us -> 199 us  [exchange(): exchange_call(True, near_send, (shaped(n_recv), shaped(n_arrived)), 3, {}...]
    reduce_sum x14 -> x0, other arithmetic: 7.12 us -> none  [the longest x6 3.17 us: count(): return jnp.sum(ind.astype(jnp.int32), axis=-1)]
    dot_general x6 -> x0, matrix products: 6.07 us -> none  [the longest x1 4.33 us: local_step(): jnp.einsum('deo,deb->dob', onehot(table // per_dev, n_dev), onehot(table...]
where the time goes in v3:
time: 410 us; the launch traced here: 409 us
  Pallas kernels  401 us (98%)
  local copies, waits for them, and re-layouts  5.63 us (1%)
    pallas_call x1, Pallas kernels, exchange(): exchange_call(True, near_send, (shaped(n_recv), shaped(n_arrived)), 3, {}...  199 us
    pallas_call x1, Pallas kernels, exchange(): exchange_call(False, far_send, shaped(n_recv), 2, {1: 0}, 'exchange_far')  117 us
    pallas_call x1, Pallas kernels, local_step(): pl.pallas_call(functools.partial(attend_kernel, cfg), out_shape=(jax.Shap...  45.6 us
    pallas_call x1, Pallas kernels, local_step(): pl.pallas_call(functools.partial(pack_pool_kernel, (per_dev, n_half, pair...  18.3 us
    pallas_call x1, Pallas kernels, local_step(): pl.pallas_call(functools.partial(plan_kernel, (n_dev, n_half, per_dev, pa...  16.5 us

profile of v3, /device:TPU:0, one launch (start us, length us, event | category | flops | bytes accessed | tf_op | source)
XLA Modules:
  0.0 408.5 jit_solution(3035881855009418857)
XLA Ops:
  0.6 0.9 copy.16
  1.6 0.1 reshape.45.table
  1.7 16.5 %plan.1 = s32[40,256]{1,0:T(8,128)S(1)} custom-call(s32[32,512]{1,0:T(8,128)S(1)} %reshape.45.table), custom_call_target="tpu_custom_call" | custom-call | tf_op jit(solution)/shard_map/plan/pallas_call | solution.py:468
  18.2 0.0 copy-start
  18.2 3.4 copy-done
  21.6 18.3 %pack_pool.1 = (bf16[640,256,128]{2,1,0:T(8,128)(2,1)}, bf16[256,256,128]{2,1,0:T(8,128)(2,1)}, bf16[8,256,128]{2,1,0:T(8,128)(2,1)S(1)}) custom-call(s32[40,256]{1,0:T(8,128)S(1)} %plan.1, bf16[256,128,128]{2,1,0:T(8,128)(2,1)S(1)} %bitcast.12, bf16[256,128,128]{2,1,0:T(8,128)(2,1)} %bitcast.13), custom_call_target="tpu_custom_call" | custom-call | tf_op jit(solution)/shard_map/pack_pool/pallas_call | solution.py:487
  39.9 0.5 slice.4
  41.1 0.0 copy-start.1
  41.1 320.9 %conditional.1 = (bf16[1536,256,128]{2,1,0:T(8,128)(2,1)}) conditional(s32[]{:T(128)} %bitcast.3, (bf16[640,256,128]{2,1,0:T(8,128)(2,1)}, bf16[256,256,128]{2,1,0:T(8,128)(2,1)}, bf16[8,256,128]{2,1,0:T(8,128)(2,1)S(1)}, s32[40,256]{1,0:T(8,128)S(1)}) %tuple.20, (bf16[640,256,128]{2,1,0:T(8,128)(2,1)}, ...), branch_computations={%region_0.0_spmd, %region_1.0_spmd, %region_2.0_spmd, %region_3.0_... | conditional | bytes 8 | solution.py:536
  41.1 198.6 %exchange_near.4 = (bf16[1536,256,128]{2,1,0:T(8,128)(2,1)}, bf16[74,256,128]{2,1,0:T(8,128)(2,1)S(1)}) custom-call(bf16[640,256,128]{2,1,0:T(8,128)(2,1)} %get-tuple-element.33.refs_0_, bf16[256,256,128]{2,1,0:T(8,128)(2,1)} %get-tuple-element.34.refs_1_, bf16[8,256,128]{2,1,0:T(8,128)(2,1)S(1)} %get-tuple-element.40.refs_2_), custom_call_target="tpu_custom_call" | custom-call | tf_op jit(solution)/shard_map/cond/branch_0_fun/exchange_near/pallas_call | solution.py:523
  239.7 5.5 %pack_relay.4.refs_0_ = bf16[896,256,128]{2,1,0:T(8,128)(2,1)} custom-call(s32[40,256]{1,0:T(8,128)S(1)} %get-tuple-element.32.plan, bf16[74,256,128]{2,1,0:T(8,128)(2,1)S(1)} %get-tuple-element.41.arrived), custom_call_target="tpu_custom_call" | custom-call | tf_op jit(solution)/shard_map/cond/branch_0_fun/pack_relay/pallas_call | solution.py:525
  245.2 116.6 %exchange_far.4 = bf16[1536,256,128]{2,1,0:T(8,128)(2,1)} custom-call(bf16[896,256,128]{2,1,0:T(8,128)(2,1)} %pack_relay.4.refs_0_, bf16[1536,256,128]{2,1,0:T(8,128)(2,1)} %get-tuple-element.42.refs_1_), custom_call_target="tpu_custom_call", output_to_operand_aliasing={{}: (1, {})} | custom-call | tf_op jit(solution)/shard_map/cond/branch_0_fun/exchange_far/pallas_call | solution.py:533
  362.0 0.0 copy-done.1
  362.0 0.1 copy.17
  362.1 0.6 reshape.46.targets
  362.7 45.6 %attend.1 = (bf16[8,1024,128]{2,1,0:T(8,128)(2,1)}, bf16[256,128,128]{2,1,0:T(8,128)(2,1)}, bf16[256,128,128]{2,1,0:T(8,128)(2,1)}) custom-call(s32[40,256]{1,0:T(8,128)S(1)} %plan.1, s32[16]{0:T(128)} %reshape.46.targets, bf16[8,1024,128]{2,1,0:T(8,128)(2,1)} %bitcast.15, bf16[8,256,128]{2,1,0:T(8,128)(2,1)} %bitcast.16, bf16[8,256,128]{2,1,0:T(8,128)(2,1)} %bitcast.18, ...), custom_call_target="tpu_custom_call" | custom-call | tf_op jit(solution)/shard_map/attend/pallas_call | solution.py:542
Async XLA Ops:
  18.2 3.4 copy-start
  41.1 321.0 %copy-start.1 = (s32[8,2]{0,1:T(2,128)S(1)}, s32[8,2]{0,1:T(2,128)}, u32[]{:S(2)}) copy-start(s32[8,2]{0,1:T(2,128)} %param.17) | copy-start | bytes 196

commit v4 on v3

--- a/solution.py
+++ b/solution.py
@@ -10,13 +10,15 @@
 F32 = jnp.float32
 BF16 = jnp.bfloat16
 ROW_CAP = 5
-POOL_CHUNK = 16
+FIND_STEP = 4
+PIECE = 32
 HOT_CAP = 64
 PLANES = 4
 HOT_PART = 4
 HOT_IN = PLANES * HOT_PART
 NEAR_ROW, RELAY_ROW, CROSS_ROW, HOT_ROW, LEVEL_ROW, POS_ROW, PLAN_ROWS = 0, 16, 32, 33, 35, 36, 40
 COUNT_LANE = 128
+LIST_LANES = 64
 MESH = pl.DeviceIdType.MESH
 ORDER = (14, 8, 4, 6, 12, 10, 2, 15, 9, 5, 7, 13, 11, 3, 1)
 LEVELS = ((8, 58, 10), (8, 64, 10), (12, 80, 16))
@@ -50,8 +52,21 @@
     return flag(src_of_row(iota((n, n), 0)) == iota((n, n), 1)).astype(BF16)
 
 
-def plan_kernel(cfg, table, out, want_s, key_s, hot_s, count_s, union_s):
-    n_dev, n_half, per_dev, pair_cap, far_cap, far_base, levels = cfg
+def plan_kernel(cfg, table, k_pool, v_pool, out, x_near, x_cross, x_hot,
+                want_s, key_s, hot_s, count_s, union_s, raw, head_major, plan, in_sem, plan_sem, out_sem):
+    n_dev, n_half, per_dev, pair_cap, far_cap, far_base, block_len, kv_heads, levels = cfg
+    n_group = n_dev // FIND_STEP
+    group_blocks = per_dev // n_group
+    perm = permutation(block_len * kv_heads, lambda r: lax.rem(r, block_len) * kv_heads + r // block_len)
+
+    def group_copies(group):
+        rows = pl.ds(group * group_blocks, group_blocks)
+        return [pltpu.make_async_copy(src.at[rows], raw.at[i, rows], in_sem.at[i, group])
+                for i, src in enumerate((k_pool, v_pool))]
+
+    for group in range(n_group):
+        for copy in group_copies(group):
+            copy.start()
     n_cols = n_dev // PLANES
     n_entry = table.shape[1]
     me = lax.axis_index('pool')
@@ -73,7 +88,19 @@
         want = flag(hits > 0)
         want_s[dest] = want
         return popular + want
-    popular = lax.fori_loop(0, n_dev, find, jnp.zeros((n_dev, per_dev), F32))
+
+    def find_and_turn(group, popular):
+        for copy in group_copies(group):
+            copy.wait()
+        for i in range(FIND_STEP):
+            popular = find(group * FIND_STEP + i, popular)
+            for j in range(group_blocks // FIND_STEP):
+                block = group * group_blocks + i * (group_blocks // FIND_STEP) + j
+                turned = dot_nn(perm, jnp.concatenate([raw[0, block], raw[1, block]], axis=1)).astype(BF16)
+                head_major[block, 0:128, :] = turned[:, 0:128]
+                head_major[block, 128:256, :] = turned[:, 128:256]
+        return popular
+    popular = lax.fori_loop(0, n_group, find_and_turn, jnp.zeros((n_dev, per_dev), F32))
 
     def search(_, bounds):
         low, high = bounds
@@ -109,7 +136,12 @@
 
     def rank_half(first, maxima):
         zero = jnp.zeros((n_dev, per_dev), F32)
-        return lax.fori_loop(first, first + n_half, rank_rest, (zero,) + maxima)
+
+        def several(step, carry):
+            for i in range(FIND_STEP):
+                carry = rank_rest(first + step * FIND_STEP + i, carry)
+            return carry
+        return lax.fori_loop(0, n_half // FIND_STEP, several, (zero,) + maxima)
     union0, pair_max, far_max = rank_half(0, (jnp.zeros((n_dev, 1), F32), jnp.zeros((n_half, 1), F32)))
     union1, pair_max, far_max = rank_half(n_half, (pair_max, far_max))
     for h, union in enumerate((union0, union1)):
@@ -123,18 +155,18 @@
     out[LEVEL_ROW:LEVEL_ROW + 1, :] = jnp.full((1, per_dev), level, jnp.int32)
 
     def compact(keys, values, size):
-        place = iota((per_dev, size), 1).astype(F32)
-        total = 0
-        for key, value in zip(keys, values):
-            total = total + jnp.sum(jnp.where(key == place, value, 0.0), axis=0, keepdims=True)
-        return total
+        places = iota((size, per_dev), 0).astype(F32)
+        hits = jnp.concatenate([flag(key == places).astype(BF16) for key in keys], axis=1)
+        values = jnp.broadcast_to(jnp.concatenate(values, axis=1), (8, per_dev * len(keys))).astype(BF16)
+        ids = lax.dot_general(values, hits, (((1,), (1,)), ((), ())), preferred_element_type=F32)
+        return ids[0:1]
 
     def put(row, ids, num):
         out[row:row + 1, 0:ids.shape[1]] = ids.astype(jnp.int32)
         if ids.shape[1] < per_dev:
             out[row:row + 1, COUNT_LANE:] = jnp.broadcast_to(num, (1, per_dev - COUNT_LANE)).astype(jnp.int32)
 
-    ids = iota((per_dev, 1), 0).astype(F32)
+    ids = iota((1, per_dev), 1).astype(F32)
     dests = [half * n_half + d for d in range(n_half)]
     stack = lambda ref, at: jnp.concatenate([ref[d, pl.ds(at, 1), :] for d in dests], axis=0)
     near_keys = stack(key_s, me)
@@ -146,26 +178,20 @@
         before = sum(relay_num)
         relay_keys.append(jnp.where(here > 0, dot_nn(here, tri) + before, -1.0))
         relay_num.append(rowsum(here))
-    relay_at = [HOT_IN + union_s[half, pl.ds(partner, 1), :]]
+    relay_at = [union_s[half, pl.ds(partner, 1), :]]
     for q in range(PLANES):
         relay_at.append(q * HOT_PART + hot_s[2, pl.ds(q * n_cols + col, 1), :])
     cross_key = union_s[1 - half, pl.ds(me, 1), :]
     hot_keys = [jnp.where(hot_s[p, pl.ds(me, 1), :] > 0, hot_s[2, pl.ds(me, 1), :], -1.0) for p in range(2)]
-    rows = [near_keys] + relay_keys + relay_at + [cross_key] + hot_keys
-    used = sum(r.shape[0] for r in rows)
-    turned = jnp.concatenate(rows + [jnp.zeros((128 - used, per_dev), F32)], axis=0).T
-    column = lambda i: turned[:, i:i + 1]
-    at0 = n_half * (PLANES + 2)
-    values = [column(at0 + q) for q in range(PLANES + 1)]
     near_num = rowsum(flag(near_keys >= 0))
     for d in range(n_half):
-        put(NEAR_ROW + d, compact([column(d)], [ids], 128), near_num[d:d + 1])
-        keys = [column(n_half * (q + 1) + d) for q in range(PLANES + 1)]
-        put(RELAY_ROW + d, compact(keys, values, 128), sum(relay_num)[d:d + 1])
-    last = at0 + PLANES + 1
-    put(CROSS_ROW, compact([column(last)], [ids], per_dev), None)
+        put(NEAR_ROW + d, compact([near_keys[d:d + 1]], [ids], LIST_LANES), near_num[d:d + 1])
+        listed = compact([keys[d:d + 1] for keys in relay_keys], relay_at, LIST_LANES)
+        from_partner = flag(iota((1, LIST_LANES), 1).astype(F32) < relay_num[0][d:d + 1])
+        put(RELAY_ROW + d, listed + HOT_IN * from_partner, sum(relay_num)[d:d + 1])
+    put(CROSS_ROW, compact([cross_key], [ids], per_dev), None)
     for p in range(2):
-        put(HOT_ROW + p, compact([column(last + 1 + p)], [ids], 128), rowsum(flag(hot_keys[p] >= 0)))
+        put(HOT_ROW + p, compact([hot_keys[p]], [ids], LIST_LANES), rowsum(flag(hot_keys[p] >= 0)))
     cross_num = rowsum(flag(cross_key >= 0)).astype(jnp.int32)
     out[LEVEL_ROW:LEVEL_ROW + 1, COUNT_LANE:] = jnp.broadcast_to(cross_num, (1, per_dev - COUNT_LANE))
 
@@ -194,38 +220,9 @@
     for i in range(n_entry // per_dev):
         out[POS_ROW + i:POS_ROW + i + 1, :] = pos[:, i * per_dev:(i + 1) * per_dev]
 
-
-def pack_pool_kernel(cfg, plan, k_pool, v_pool, x_near, x_cross, x_hot, raw, head_major, in_sem, out_sem):
-    per_dev, n_half, pair_cap, block_len, kv_heads = cfg
-    n_chunk = per_dev // POOL_CHUNK
-    perm = permutation(block_len * kv_heads, lambda r: lax.rem(r, block_len) * kv_heads + r // block_len)
-
-    def chunk_copies(chunk, slot):
-        rows = pl.ds(chunk * POOL_CHUNK, POOL_CHUNK)
-        return (pltpu.make_async_copy(k_pool.at[rows], raw.at[slot, 0], in_sem.at[slot, 0]),
-                pltpu.make_async_copy(v_pool.at[rows], raw.at[slot, 1], in_sem.at[slot, 1]))
-
-    for copy in chunk_copies(0, 0):
-        copy.start()
-
-    def turn_chunk(chunk, carry):
-        slot = lax.rem(chunk, 2)
-
-        @pl.when(chunk + 1 < n_chunk)
-        def _():
-            for copy in chunk_copies(chunk + 1, 1 - slot):
-                copy.start()
-
-        for copy in chunk_copies(chunk, slot):
-            copy.wait()
-        for j in range(POOL_CHUNK):
-            both = jnp.concatenate([raw[slot, 0, j], raw[slot, 1, j]], axis=1)
-            turned = jnp.dot(perm, both, preferred_element_type=F32).astype(BF16)
-            head_major[chunk * POOL_CHUNK + j, 0:128, :] = turned[:, 0:128]
-            head_major[chunk * POOL_CHUNK + j, 128:256, :] = turned[:, 128:256]
-        return carry
-
-    lax.fori_loop(0, n_chunk, turn_chunk, 0)
+    to_scalar = pltpu.make_async_copy(out, plan, plan_sem)
+    to_scalar.start()
+    to_scalar.wait()
 
     def start_list(row, count, dest, base):
         def body(k, carry):
@@ -236,13 +233,13 @@
     total = plan[LEVEL_ROW, COUNT_LANE]
     start_list(CROSS_ROW, total, x_cross, 0)
     for q in range(2):
-        num = plan[HOT_ROW + q, COUNT_LANE]
-        start_list(HOT_ROW + q, num, x_hot, q * HOT_PART)
-        total = total + num
+        count = plan[HOT_ROW + q, COUNT_LANE]
+        start_list(HOT_ROW + q, count, x_hot, q * HOT_PART)
+        total = total + count
     for q in range(n_half):
-        num = plan[NEAR_ROW + q, COUNT_LANE]
-        start_list(NEAR_ROW + q, num, x_near, q * pair_cap)
-        total = total + num
+        count = plan[NEAR_ROW + q, COUNT_LANE]
+        start_list(NEAR_ROW + q, count, x_near, q * pair_cap)
+        total = total + count
 
     def drain(k, carry):
         pltpu.make_async_copy(head_major.at[0], x_near.at[0], out_sem).wait()
@@ -332,7 +329,7 @@
 
 
 def attend_kernel(cfg, plan, targets, q_ref, kn_ref, vn_ref, recv, k_pool, v_pool, k_new, v_new,
-                  out_ref, k_out, v_out, kv, q_heads, heads_out, sem, pool_buf, new_buf, pool_in, pool_done, new_sem):
+                  out_ref, k_out, v_out, kv, q_heads, heads_out, new_heads_kv, s_pref, s_self, p_pref, p_self, sem, pool_buf, new_buf, pool_in, pool_done, new_sem):
     n_pref, block_len, kv_heads, groups, chunk_len, head_dim, n_req, per_dev, n_new = cfg
     req = pl.program_id(0)
     slot = lax.rem(req, 2)
@@ -340,11 +337,10 @@
     piece = 2 * per_dev // n_req
     per_row = per_dev // n_pref
 
-    def fetch(which, into):
-        def body(k, carry):
-            pltpu.make_async_copy(recv.at[plan[POS_ROW + which // per_row, lax.rem(which, per_row) * n_pref + k]], kv.at[into, k], sem.at[into]).start()
-            return carry
-        lax.fori_loop(0, n_pref, body, 0, unroll=8)
+    def fetch(which, into, first, num):
+        row, lane = POS_ROW + which // per_row, lax.rem(which, per_row) * n_pref
+        for k in range(num):
+            pltpu.make_async_copy(recv.at[plan[row, lane + first + k]], kv.at[into, first + k], sem.at[into]).start()
 
     def pool_copies(step, at):
         rows = pl.ds(step * piece, piece)
@@ -362,13 +358,9 @@
 
     @pl.when(req == 0)
     def _():
-        fetch(0, 0)
+        fetch(0, 0, 0, n_pref)
         for copy in pool_copies(0, 0)[0] + new_in:
             copy.start()
-
-    @pl.when(req + 1 < n_req)
-    def _():
-        fetch(req + 1, 1 - slot)
 
     n_step = n_req // 2
     for step in range(n_step):
@@ -404,7 +396,11 @@
             new_out(i, 0).wait()
             new_out(i, 1).wait()
 
-    pltpu.make_async_copy(recv.at[pl.ds(0, n_pref)], kv.at[slot], sem.at[slot]).wait()
+    def whole_request(at):
+        return pltpu.make_async_copy(recv.at[pl.ds(0, n_pref)], kv.at[at], sem.at[at])
+
+    whole_request(slot).wait()
+    aligned = lambda i, n: pl.multiple_of(i * n, n)
 
     rows = chunk_len * groups
     token = lax.broadcasted_iota(jnp.int32, (rows, chunk_len), 0) // groups
@@ -423,30 +419,60 @@
         for h in range(kv_heads):
             q_heads[h, g * span:(g + 1) * span, :] = part[h * span:(h + 1) * span]
     new_kv = jnp.concatenate([kn_ref[0], vn_ref[0]], axis=1)
-    new_kv = jnp.dot(new_heads, new_kv, preferred_element_type=F32).astype(BF16)
-    for h in range(kv_heads):
-        q_h = q_heads[h]
-        k_own = new_kv[h * chunk_len:(h + 1) * chunk_len, 0:head_dim]
-        v_own = new_kv[h * chunk_len:(h + 1) * chunk_len, head_dim:]
-        k_h = kv[slot, :, h * block_len:(h + 1) * block_len, :].reshape(n_keys, head_dim)
-        v_at = (kv_heads + h) * block_len
-        v_h = kv[slot, :, v_at:v_at + block_len, :].reshape(n_keys, head_dim)
-        s_pref = lax.dot_general(q_h, k_h, nt, preferred_element_type=F32)
-        s_self = lax.dot_general(q_h, k_own, nt, preferred_element_type=F32)
-        s_self = jnp.where(causal, s_self, -jnp.inf)
-        row_max = jnp.maximum(jnp.max(s_pref, axis=-1, keepdims=True), jnp.max(s_self, axis=-1, keepdims=True))
-        e_pref = jnp.exp2((s_pref - row_max) * exp_scale)
-        e_self = jnp.exp2((s_self - row_max) * exp_scale)
-        total = jnp.sum(e_pref, axis=-1, keepdims=True) + jnp.sum(e_self, axis=-1, keepdims=True)
-        inv = 1.0 / total
-        p_pref = (e_pref * inv).astype(BF16)
-        p_self = (e_self * inv).astype(BF16)
-        acc = jnp.dot(p_pref, v_h, preferred_element_type=F32)
-        acc = acc + jnp.dot(p_self, v_own, preferred_element_type=F32)
+    new_heads_kv[...] = jnp.dot(new_heads, new_kv, preferred_element_type=F32).astype(BF16)
+    def scores(h, at):
+        k_h = kv[slot, :, pl.ds(aligned(h, block_len), block_len), :].reshape(n_keys, head_dim)
+        k_own = new_heads_kv[pl.ds(aligned(h, chunk_len), chunk_len), 0:head_dim]
+        s_pref[at] = lax.dot_general(q_heads[h], k_h, nt, preferred_element_type=F32)
+        s_own = lax.dot_general(q_heads[h], k_own, nt, preferred_element_type=F32)
+        s_self[at] = jnp.where(causal, s_own, -jnp.inf)
+
+    def probabilities(h, at):
+        for first in range(0, rows, PIECE):
+            part = pl.ds(first, PIECE)
+            far, own = s_pref[at, part], s_self[at, part]
+            row_max = jnp.maximum(jnp.max(far, axis=-1, keepdims=True), jnp.max(own, axis=-1, keepdims=True))
+            far = jnp.exp2((far - row_max) * exp_scale)
+            own = jnp.exp2((own - row_max) * exp_scale)
+            inv = 1.0 / (jnp.sum(far, axis=-1, keepdims=True) + jnp.sum(own, axis=-1, keepdims=True))
+            p_pref[at, part] = (far * inv).astype(BF16)
+            p_self[at, part] = (own * inv).astype(BF16)
+
+    def values(h, at):
+        v_h = kv[slot, :, pl.ds(aligned(kv_heads + h, block_len), block_len), :].reshape(n_keys, head_dim)
+        v_own = new_heads_kv[pl.ds(aligned(h, chunk_len), chunk_len), head_dim:]
+        acc = jnp.dot(p_pref[at], v_h, preferred_element_type=F32)
+        acc = acc + jnp.dot(p_self[at], v_own, preferred_element_type=F32)
         heads_out[h] = acc.astype(BF16)
+
+    n_part = n_pref // kv_heads
+    after = jnp.minimum(req + 1, n_req - 1)
+
+    fetch(after, 1 - slot, 0, n_part)
+    scores(0, 0)
+    fetch(after, 1 - slot, n_part, n_part)
+    scores(1, 1)
+    probabilities(0, 0)
+
+    def steady(pair, carry):
+        for at in range(2):
+            h = 2 * pair + at
+            fetch(after, 1 - slot, h * n_part, n_part)
+            scores(h, at)
+            probabilities(h - 1, 1 - at)
+            values(h - 2, at)
+        return carry
+    lax.fori_loop(1, kv_heads // 2, steady, 0)
+    probabilities(kv_heads - 1, 1)
+    values(kv_heads - 2, 0)
+    values(kv_heads - 1, 1)
     for g in range(rows // span):
         part = heads_out[:, g * span:(g + 1) * span, :].reshape(256, head_dim)
         out_ref[0, g * 256:(g + 1) * 256, :] = jnp.dot(to_tokens, part, preferred_element_type=F32).astype(BF16)
+
+    @pl.when(req == n_req - 1)
+    def _():
+        whole_request(1 - slot).wait()
 
 
 def solution(mesh):
@@ -461,45 +487,38 @@
         block_rows = block_len * kv_heads
         pair_cap = req_count * ROW_CAP
         n_half = n_dev // 2
+        rows = chunk_len * groups
         n_cols = n_dev // PLANES
         far_cap = pair_cap + HOT_IN
         far_base = n_half * pair_cap
         n_recv = far_base + n_half * far_cap
-        plan = pl.pallas_call(
-            functools.partial(plan_kernel, (n_dev, n_half, per_dev, pair_cap, far_cap, far_base, LEVELS)),
-            out_shape=jax.ShapeDtypeStruct((PLAN_ROWS, per_dev), jnp.int32),
-            in_specs=[vmem_spec()], out_specs=vmem_spec(),
+        block_shape = (2 * block_rows, head_dim)
+        shaped = lambda n: jax.ShapeDtypeStruct((n,) + block_shape, BF16)
+        flat_pool = (per_dev, block_rows, head_dim)
+        k_flat, v_flat = k_pool.reshape(flat_pool), v_pool.reshape(flat_pool)
+        plan, x_near, x_cross, x_hot = pl.pallas_call(
+            functools.partial(plan_kernel, (n_dev, n_half, per_dev, pair_cap, far_cap, far_base, block_len,
+                                            kv_heads, LEVELS)),
+            out_shape=(jax.ShapeDtypeStruct((PLAN_ROWS, per_dev), jnp.int32),
+                       shaped(n_half * pair_cap), shaped(per_dev), shaped(2 * HOT_PART)),
+            in_specs=[vmem_spec()] + [any_spec()] * 2, out_specs=(vmem_spec(),) + (any_spec(),) * 3,
             scratch_shapes=[
                 pltpu.VMEM((n_dev, n_dev, per_dev), F32),
                 pltpu.VMEM((n_dev, n_dev, per_dev), F32),
                 pltpu.VMEM((3, n_dev, per_dev), F32),
                 pltpu.VMEM((n_dev, n_dev, 128), F32),
                 pltpu.VMEM((2, n_dev, per_dev), F32),
-            ],
-            compiler_params=pltpu.CompilerParams(vmem_limit_bytes=24 << 20),
-            name='plan',
-        )(block_table.reshape(n_dev, req_count * n_pref))
-
-        block_shape = (2 * block_rows, head_dim)
-        shaped = lambda n: jax.ShapeDtypeStruct((n,) + block_shape, BF16)
-        flat_pool = (per_dev, block_rows, head_dim)
-        k_flat, v_flat = k_pool.reshape(flat_pool), v_pool.reshape(flat_pool)
-        x_near, x_cross, x_hot = pl.pallas_call(
-            functools.partial(pack_pool_kernel, (per_dev, n_half, pair_cap, block_len, kv_heads)),
-            out_shape=(shaped(n_half * pair_cap), shaped(per_dev), shaped(2 * HOT_PART)),
-            in_specs=[smem_spec()] + [any_spec()] * 2,
-            out_specs=(any_spec(),) * 3,
-            scratch_shapes=[
-                pltpu.VMEM((2, 2, POOL_CHUNK, block_rows, head_dim), BF16),
+                pltpu.VMEM((2,) + flat_pool, BF16),
                 pltpu.VMEM((per_dev,) + block_shape, BF16),
-                pltpu.SemaphoreType.DMA((2, 2)),
+                pltpu.SMEM((PLAN_ROWS, per_dev), jnp.int32),
+                pltpu.SemaphoreType.DMA((2, n_dev // FIND_STEP)),
+                pltpu.SemaphoreType.DMA,
                 pltpu.SemaphoreType.DMA,
             ],
-            compiler_params=pltpu.CompilerParams(vmem_limit_bytes=40 << 20),
-            name='pack_pool',
-        )(plan, k_flat, v_flat)
-
-        rows = chunk_len * groups
+            compiler_params=pltpu.CompilerParams(vmem_limit_bytes=56 << 20),
+            name='plan',
+        )(block_table.reshape(n_dev, req_count * n_pref), k_flat, v_flat)
+
         def exchange(level, near_send, n_cross, far_send, x_near, x_cross, x_hot, plan):
             n_arrived = HOT_IN + n_cross
 
@@ -553,6 +572,11 @@
                 pltpu.VMEM((2, n_pref) + block_shape, BF16),
                 pltpu.VMEM((kv_heads, rows, head_dim), BF16),
                 pltpu.VMEM((kv_heads, rows, head_dim), BF16),
+                pltpu.VMEM((chunk_len * kv_heads, 2 * head_dim), BF16),
+                pltpu.VMEM((2, rows, n_pref * block_len), F32),
+                pltpu.VMEM((2, rows, chunk_len), F32),
+                pltpu.VMEM((2, rows, n_pref * block_len), BF16),
+                pltpu.VMEM((2, rows, chunk_len), BF16),
                 pltpu.SemaphoreType.DMA((2,)),
                 pltpu.VMEM((2, 2, 2 * per_dev // req_count, block_rows, head_dim), BF16),
                 pltpu.VMEM((2,) + new_shape, BF16),

time: 410 us -> 384 us (0.937)
  Pallas kernels: 401 us -> 379 us
    pallas_call x1 -> x0, Pallas kernels: 18.3 us -> none  [local_step(): pl.pallas_call(functools.partial(pack_pool_kernel, (per_dev, n_half, pair...]
    pallas_call x1, Pallas kernels: 45.6 us -> 38.2 us  [local_step(): pl.pallas_call(functools.partial(attend_kernel, cfg), out_shape=(jax.Shap...]
where the time goes in v4:
time: 384 us; the launch traced here: 383 us
  Pallas kernels  379 us (99%)
    pallas_call x1, Pallas kernels, exchange(): exchange_call(True, near_send, (shaped(n_recv), shaped(n_arrived)), 3, {}...  198 us
    pallas_call x1, Pallas kernels, exchange(): exchange_call(False, far_send, shaped(n_recv), 2, {1: 0}, 'exchange_far')  117 us
    pallas_call x1, Pallas kernels, local_step(): pl.pallas_call(functools.partial(attend_kernel, cfg), out_shape=(jax.Shap...  38.2 us
    pallas_call x1, Pallas kernels, local_step(): pl.pallas_call(functools.partial(plan_kernel, (n_dev, n_half, per_dev, pa...  19.6 us

profile of v4, /device:TPU:0, one launch (start us, length us, event | category | flops | bytes accessed | tf_op | source)
XLA Modules:
  0.0 382.8 jit_solution(9597711054651697627)
XLA Ops:
  0.6 0.9 copy.16
  1.6 0.7 reshape.45.table
  2.3 19.6 %plan.1 = (s32[40,256]{1,0:T(8,128)S(1)}, bf16[640,256,128]{2,1,0:T(8,128)(2,1)}, bf16[256,256,128]{2,1,0:T(8,128)(2,1)}, bf16[8,256,128]{2,1,0:T(8,128)(2,1)S(1)}) custom-call(s32[32,512]{1,0:T(8,128)} %reshape.45.table, bf16[256,128,128]{2,1,0:T(8,128)(2,1)} %bitcast.11, bf16[256,128,128]{2,1,0:T(8,128)(2,1)} %bitcast.13), custom_call_target="tpu_custom_call" | custom-call | tf_op jit(solution)/shard_map/plan/pallas_call | solution.py:499
  21.9 0.5 slice.3
  23.1 0.0 copy-start
  23.1 320.8 %conditional.1 = (bf16[1536,256,128]{2,1,0:T(8,128)(2,1)}) conditional(s32[]{:T(128)} %bitcast.5, (bf16[640,256,128]{2,1,0:T(8,128)(2,1)}, bf16[256,256,128]{2,1,0:T(8,128)(2,1)}, bf16[8,256,128]{2,1,0:T(8,128)(2,1)S(1)}, s32[40,256]{1,0:T(8,128)S(1)}) %tuple.20, (bf16[640,256,128]{2,1,0:T(8,128)(2,1)}, ...), branch_computations={%region_0.0_spmd, %region_1.0_spmd, %region_2.0_spmd, %region_3.0_... | conditional | bytes 8 | solution.py:555
  23.1 198.5 %exchange_near.4 = (bf16[1536,256,128]{2,1,0:T(8,128)(2,1)}, bf16[74,256,128]{2,1,0:T(8,128)(2,1)S(1)}) custom-call(bf16[640,256,128]{2,1,0:T(8,128)(2,1)} %get-tuple-element.33.refs_0_, bf16[256,256,128]{2,1,0:T(8,128)(2,1)} %get-tuple-element.34.refs_1_, bf16[8,256,128]{2,1,0:T(8,128)(2,1)S(1)} %get-tuple-element.40.refs_2_), custom_call_target="tpu_custom_call" | custom-call | tf_op jit(solution)/shard_map/cond/branch_0_fun/exchange_near/pallas_call | solution.py:542
  221.6 5.6 %pack_relay.4.refs_0_ = bf16[896,256,128]{2,1,0:T(8,128)(2,1)} custom-call(s32[40,256]{1,0:T(8,128)S(1)} %get-tuple-element.32.plan, bf16[74,256,128]{2,1,0:T(8,128)(2,1)S(1)} %get-tuple-element.41.arrived), custom_call_target="tpu_custom_call" | custom-call | tf_op jit(solution)/shard_map/cond/branch_0_fun/pack_relay/pallas_call | solution.py:544
  227.2 116.6 %exchange_far.4 = bf16[1536,256,128]{2,1,0:T(8,128)(2,1)} custom-call(bf16[896,256,128]{2,1,0:T(8,128)(2,1)} %pack_relay.4.refs_0_, bf16[1536,256,128]{2,1,0:T(8,128)(2,1)} %get-tuple-element.42.refs_1_), custom_call_target="tpu_custom_call", output_to_operand_aliasing={{}: (1, {})} | custom-call | tf_op jit(solution)/shard_map/cond/branch_0_fun/exchange_far/pallas_call | solution.py:552
  343.9 0.0 copy-done
  343.9 0.1 copy.17
  344.0 0.6 reshape.48.targets
  344.6 38.2 %attend.1 = (bf16[8,1024,128]{2,1,0:T(8,128)(2,1)}, bf16[256,128,128]{2,1,0:T(8,128)(2,1)}, bf16[256,128,128]{2,1,0:T(8,128)(2,1)}) custom-call(s32[40,256]{1,0:T(8,128)S(1)} %get-tuple-element.71.plan, s32[16]{0:T(128)} %reshape.48.targets, bf16[8,1024,128]{2,1,0:T(8,128)(2,1)} %bitcast.15, bf16[8,256,128]{2,1,0:T(8,128)(2,1)} %bitcast.16, ...), custom_call_target="tpu_custom_call" | custom-call | tf_op jit(solution)/shard_map/attend/pallas_call | solution.py:561
Async XLA Ops:
  23.1 320.8 %copy-start = (s32[8,2]{0,1:T(2,128)S(1)}, s32[8,2]{0,1:T(2,128)}, u32[]{:S(2)}) copy-start(s32[8,2]{0,1:T(2,128)} %param.17) | copy-start | bytes 196

commit v5 on v4

--- a/solution.py
+++ b/solution.py
@@ -21,7 +21,7 @@
 LIST_LANES = 64
 MESH = pl.DeviceIdType.MESH
 ORDER = (14, 8, 4, 6, 12, 10, 2, 15, 9, 5, 7, 13, 11, 3, 1)
-LEVELS = ((8, 58, 10), (8, 64, 10), (12, 80, 16))
+LEVELS = ((8, 54, 10), (8, 56, 10), (8, 58, 10), (8, 61, 10), (8, 64, 10), (12, 80, 16))
 
 
 def any_spec():
@@ -52,9 +52,10 @@
     return flag(src_of_row(iota((n, n), 0)) == iota((n, n), 1)).astype(BF16)
 
 
-def plan_kernel(cfg, table, k_pool, v_pool, out, x_near, x_cross, x_hot,
-                want_s, key_s, hot_s, count_s, union_s, raw, head_major, plan, in_sem, plan_sem, out_sem):
-    n_dev, n_half, per_dev, pair_cap, far_cap, far_base, block_len, kv_heads, levels = cfg
+def plan_kernel(cfg, targets, table_in, k_pool, v_pool, k_new, v_new, out, x_near, x_cross, x_hot, k_out, v_out,
+                by_row, table, want_s, key_s, hot_s, count_s, union_s, raw, head_major, plan, new_buf,
+                in_sem, pool_sem, new_sem, plan_sem, out_sem):
+    n_dev, n_half, per_dev, pair_cap, far_cap, far_base, block_len, kv_heads, n_new, levels = cfg
     n_group = n_dev // FIND_STEP
     group_blocks = per_dev // n_group
     perm = permutation(block_len * kv_heads, lambda r: lax.rem(r, block_len) * kv_heads + r // block_len)
@@ -64,11 +65,19 @@
         return [pltpu.make_async_copy(src.at[rows], raw.at[i, rows], in_sem.at[i, group])
                 for i, src in enumerate((k_pool, v_pool))]
 
+    new_in = [pltpu.make_async_copy(src, new_buf.at[i], new_sem.at[i]) for i, src in enumerate((k_new, v_new))]
+    pool_out = [pltpu.make_async_copy(raw.at[i], dst, pool_sem.at[i]) for i, dst in enumerate((k_out, v_out))]
     for group in range(n_group):
         for copy in group_copies(group):
             copy.start()
+    for copy in new_in:
+        copy.start()
     n_cols = n_dev // PLANES
-    n_entry = table.shape[1]
+    n_pref, n_entry = table_in.shape[0], table.shape[1]
+    n_req = n_entry // n_pref
+    by_row[...] = table_in[...].T
+    for r in range(n_req):
+        table[:, r * n_pref:(r + 1) * n_pref] = by_row[pl.ds(r, n_dev, stride=n_req), :]
     me = lax.axis_index('pool')
     half, in_half = me // n_half, lax.rem(me, n_half)
     partner = (1 - half) * n_half + in_half
@@ -101,6 +110,8 @@
                 head_major[block, 128:256, :] = turned[:, 128:256]
         return popular
     popular = lax.fori_loop(0, n_group, find_and_turn, jnp.zeros((n_dev, per_dev), F32))
+    for copy in pool_out:
+        copy.start()
 
     def search(_, bounds):
         low, high = bounds
@@ -241,10 +252,24 @@
         start_list(NEAR_ROW + q, count, x_near, q * pair_cap)
         total = total + count
 
+    for copy in pool_out + new_in:
+        copy.wait()
+
+    def new_copies(i):
+        return [pltpu.make_async_copy(new_buf.at[which, i], dst.at[targets[i % targets.shape[0], i // targets.shape[0]]], new_sem.at[which])
+                for which, dst in enumerate((k_out, v_out))]
+
+    for i in range(n_new):
+        for copy in new_copies(i):
+            copy.start()
+
     def drain(k, carry):
         pltpu.make_async_copy(head_major.at[0], x_near.at[0], out_sem).wait()
         return carry
     lax.fori_loop(0, total, drain, 0)
+    for i in range(n_new):
+        for copy in new_copies(i):
+            copy.wait()
 
 
 def pack_relay_kernel(cfg, plan, arrived, x_out, stage, in_sem, out_sem):
@@ -328,13 +353,12 @@
         copy.wait()
 
 
-def attend_kernel(cfg, plan, targets, q_ref, kn_ref, vn_ref, recv, k_pool, v_pool, k_new, v_new,
-                  out_ref, k_out, v_out, kv, q_heads, heads_out, new_heads_kv, s_pref, s_self, p_pref, p_self, sem, pool_buf, new_buf, pool_in, pool_done, new_sem):
-    n_pref, block_len, kv_heads, groups, chunk_len, head_dim, n_req, per_dev, n_new = cfg
+def attend_kernel(cfg, plan, q_ref, kn_ref, vn_ref, recv, out_ref,
+                  kv, q_heads, heads_out, new_heads_kv, s_pref, s_self, p_pref, p_self, sem):
+    n_pref, block_len, kv_heads, groups, chunk_len, head_dim, n_req, per_dev = cfg
     req = pl.program_id(0)
     slot = lax.rem(req, 2)
     exp_scale = float(head_dim ** -0.5 * 1.4426950408889634)
-    piece = 2 * per_dev // n_req
     per_row = per_dev // n_pref
 
     def fetch(which, into, first, num):
@@ -342,59 +366,9 @@
         for k in range(num):
             pltpu.make_async_copy(recv.at[plan[row, lane + first + k]], kv.at[into, first + k], sem.at[into]).start()
 
-    def pool_copies(step, at):
-        rows = pl.ds(step * piece, piece)
-        pairs = ((k_pool, k_out), (v_pool, v_out))
-        return ([pltpu.make_async_copy(src.at[rows], pool_buf.at[at, i], pool_in.at[at, i])
-                 for i, (src, _) in enumerate(pairs)],
-                [pltpu.make_async_copy(pool_buf.at[at, i], dst.at[rows], pool_done.at[at, i])
-                 for i, (_, dst) in enumerate(pairs)])
-
-    new_in = [pltpu.make_async_copy(src, new_buf.at[i], new_sem.at[i]) for i, src in enumerate((k_new, v_new))]
-
-    def new_out(i, which):
-        dst = (k_out, v_out)[which]
-        return pltpu.make_async_copy(new_buf.at[which, i], dst.at[targets[i]], new_sem.at[2])
-
     @pl.when(req == 0)
     def _():
         fetch(0, 0, 0, n_pref)
-        for copy in pool_copies(0, 0)[0] + new_in:
-            copy.start()
-
-    n_step = n_req // 2
-    for step in range(n_step):
-        @pl.when(req == step)
-        def _(step=step):
-            at = step % 2
-            ins, outs = pool_copies(step, at)
-            for copy in ins:
-                copy.wait()
-            for copy in outs:
-                copy.start()
-            if step + 1 < n_step:
-                if step > 0:
-                    for copy in pool_copies(step - 1, 1 - at)[1]:
-                        copy.wait()
-                for copy in pool_copies(step + 1, 1 - at)[0]:
-                    copy.start()
-
-    @pl.when(req == n_step)
-    def _():
-        for step in (n_step - 2, n_step - 1):
-            for copy in pool_copies(step, step % 2)[1]:
-                copy.wait()
-        for copy in new_in:
-            copy.wait()
-        for i in range(n_new):
-            new_out(i, 0).start()
-            new_out(i, 1).start()
-
-    @pl.when(req == n_req - 1)
-    def _():
-        for i in range(n_new):
-            new_out(i, 0).wait()
-            new_out(i, 1).wait()
 
     def whole_request(at):
         return pltpu.make_async_copy(recv.at[pl.ds(0, n_pref)], kv.at[at], sem.at[at])
@@ -495,14 +469,18 @@
         block_shape = (2 * block_rows, head_dim)
         shaped = lambda n: jax.ShapeDtypeStruct((n,) + block_shape, BF16)
         flat_pool = (per_dev, block_rows, head_dim)
+        new_shape = (write_ids.size, block_rows, head_dim)
         k_flat, v_flat = k_pool.reshape(flat_pool), v_pool.reshape(flat_pool)
-        plan, x_near, x_cross, x_hot = pl.pallas_call(
+        plan, x_near, x_cross, x_hot, k_pool_out, v_pool_out = pl.pallas_call(
             functools.partial(plan_kernel, (n_dev, n_half, per_dev, pair_cap, far_cap, far_base, block_len,
-                                            kv_heads, LEVELS)),
+                                            kv_heads, write_ids.size, LEVELS)),
             out_shape=(jax.ShapeDtypeStruct((PLAN_ROWS, per_dev), jnp.int32),
-                       shaped(n_half * pair_cap), shaped(per_dev), shaped(2 * HOT_PART)),
-            in_specs=[vmem_spec()] + [any_spec()] * 2, out_specs=(vmem_spec(),) + (any_spec(),) * 3,
+                       shaped(n_half * pair_cap), shaped(per_dev), shaped(2 * HOT_PART),
+                       jax.ShapeDtypeStruct(flat_pool, BF16), jax.ShapeDtypeStruct(flat_pool, BF16)),
+            in_specs=[smem_spec(), vmem_spec()] + [any_spec()] * 4, out_specs=(vmem_spec(),) + (any_spec(),) * 5,
             scratch_shapes=[
+                pltpu.VMEM(block_table.shape, jnp.int32),
+                pltpu.VMEM((n_dev, req_count * n_pref), jnp.int32),
                 pltpu.VMEM((n_dev, n_dev, per_dev), F32),
                 pltpu.VMEM((n_dev, n_dev, per_dev), F32),
                 pltpu.VMEM((3, n_dev, per_dev), F32),
@@ -511,13 +489,17 @@
                 pltpu.VMEM((2,) + flat_pool, BF16),
                 pltpu.VMEM((per_dev,) + block_shape, BF16),
                 pltpu.SMEM((PLAN_ROWS, per_dev), jnp.int32),
+                pltpu.VMEM((2,) + new_shape, BF16),
                 pltpu.SemaphoreType.DMA((2, n_dev // FIND_STEP)),
+                pltpu.SemaphoreType.DMA((2,)),
+                pltpu.SemaphoreType.DMA((2,)),
                 pltpu.SemaphoreType.DMA,
                 pltpu.SemaphoreType.DMA,
             ],
             compiler_params=pltpu.CompilerParams(vmem_limit_bytes=56 << 20),
             name='plan',
-        )(block_table.reshape(n_dev, req_count * n_pref), k_flat, v_flat)
+        )(write_ids.T, block_table.T, k_flat, v_flat,
+          k_new.reshape(new_shape), v_new.reshape(new_shape))
 
         def exchange(level, near_send, n_cross, far_send, x_near, x_cross, x_hot, plan):
             n_arrived = HOT_IN + n_cross
@@ -555,19 +537,17 @@
         recv = lax.switch(plan[LEVEL_ROW, 0], [functools.partial(exchange, i, *s) for i, s in enumerate(sizes)],
                           x_near, x_cross, x_hot, plan)
 
-        cfg = (n_pref, block_len, kv_heads, groups, chunk_len, head_dim, req_count, per_dev, write_ids.size)
-        new_shape = (write_ids.size, block_rows, head_dim)
+        cfg = (n_pref, block_len, kv_heads, groups, chunk_len, head_dim, req_count, per_dev)
         row_block = lambda *dims: pl.BlockSpec((1,) + dims, lambda r: (r,) + (0,) * len(dims))
-        attn, k_pool_out, v_pool_out = pl.pallas_call(
+        attn = pl.pallas_call(
             functools.partial(attend_kernel, cfg),
-            out_shape=(jax.ShapeDtypeStruct((req_count, chunk_len * q_heads, head_dim), BF16),
-                       jax.ShapeDtypeStruct(flat_pool, BF16), jax.ShapeDtypeStruct(flat_pool, BF16)),
+            out_shape=jax.ShapeDtypeStruct((req_count, chunk_len * q_heads, head_dim), BF16),
             grid=(req_count,),
             in_specs=[
-                smem_spec(), smem_spec(), row_block(chunk_len * q_heads, head_dim),
-                row_block(chunk_len * kv_heads, head_dim), row_block(chunk_len * kv_heads, head_dim),
-            ] + [any_spec()] * 5,
-            out_specs=(row_block(chunk_len * q_heads, head_dim), any_spec(), any_spec()),
+                smem_spec(), row_block(chunk_len * q_heads, head_dim),
+                row_block(chunk_len * kv_heads, head_dim), row_block(chunk_len * kv_heads, head_dim), any_spec(),
+            ],
+            out_specs=row_block(chunk_len * q_heads, head_dim),
             scratch_shapes=[
                 pltpu.VMEM((2, n_pref) + block_shape, BF16),
                 pltpu.VMEM((kv_heads, rows, head_dim), BF16),
@@ -578,19 +558,13 @@
                 pltpu.VMEM((2, rows, n_pref * block_len), BF16),
                 pltpu.VMEM((2, rows, chunk_len), BF16),
                 pltpu.SemaphoreType.DMA((2,)),
-                pltpu.VMEM((2, 2, 2 * per_dev // req_count, block_rows, head_dim), BF16),
-                pltpu.VMEM((2,) + new_shape, BF16),
-                pltpu.SemaphoreType.DMA((2, 2)),
-                pltpu.SemaphoreType.DMA((2, 2)),
-                pltpu.SemaphoreType.DMA((3,)),
             ],
             compiler_params=pltpu.CompilerParams(
                 vmem_limit_bytes=56 << 20, dimension_semantics=('arbitrary',)),
             name='attend',
-        )(plan, write_ids.reshape(-1), queries.reshape(req_count, chunk_len * q_heads, head_dim),
+        )(plan, queries.reshape(req_count, chunk_len * q_heads, head_dim),
           k_new.reshape(req_count, chunk_len * kv_heads, head_dim),
-          v_new.reshape(req_count, chunk_len * kv_heads, head_dim), recv, k_flat, v_flat,
-          k_new.reshape(new_shape), v_new.reshape(new_shape))
+          v_new.reshape(req_count, chunk_len * kv_heads, head_dim), recv)
         attn_out = attn.reshape(req_count, chunk_len, q_heads, head_dim)
         return attn_out, k_pool_out.reshape(k_pool.shape), v_pool_out.reshape(v_pool.shape)
 

time: 384 us -> 373 us (0.971)
  Pallas kernels: 379 us -> 372 us
    pallas_call x1, Pallas kernels: 38.2 us -> 31.2 us  [local_step(): pl.pallas_call(functools.partial(attend_kernel, cfg), out_shape=jax.Shape...]
where the time goes in v5:
time: 373 us
  Pallas kernels  372 us (100%)
    pallas_call x1, Pallas kernels, exchange(): exchange_call(True, near_send, (shaped(n_recv), shaped(n_arrived)), 3, {}...  198 us
    pallas_call x1, Pallas kernels, exchange(): exchange_call(False, far_send, shaped(n_recv), 2, {1: 0}, 'exchange_far')  117 us
    pallas_call x1, Pallas kernels, local_step(): pl.pallas_call(functools.partial(attend_kernel, cfg), out_shape=jax.Shape...  31.2 us
    pallas_call x1, Pallas kernels, local_step(): pl.pallas_call(functools.partial(plan_kernel, (n_dev, n_half, per_dev, pa...  19.9 us

profile of v5, /device:TPU:0, one launch (start us, length us, event | category | flops | bytes accessed | tf_op | source)
XLA Modules:
  0.0 373.5 jit_solution(2024937681733688205)
XLA Ops:
  0.6 19.9 %plan.1 = (s32[40,256]{1,0:T(8,128)S(1)}, bf16[640,256,128]{2,1,0:T(8,128)(2,1)}, bf16[256,256,128]{2,1,0:T(8,128)(2,1)}, bf16[8,256,128]{2,1,0:T(8,128)(2,1)S(1...) custom-call(s32[2,8]{1,0:T(2,128)} %bitcast.22, s32[64,256]{1,0:T(8,128)} %bitcast.21, ...), custom_call_target="tpu_custom_call" | custom-call | tf_op jit(solution)/shard_map/plan/pallas_call | solution.py:474
  20.5 0.5 slice.3
  21.7 320.6 %conditional.1 = (bf16[1536,256,128]{2,1,0:T(8,128)(2,1)}) conditional(s32[]{:T(128)} %bitcast.9, (bf16[640,256,128]{2,1,0:T(8,128)(2,1)}, bf16[256,256,128]{2,1,0:T(8,128)(2,1)}, bf16[8,256,128]{2,1,0:T(8,128)(2,1)S(1)}, s32[40,256]{1,0:T(8,128)S(1)}) %tuple.29, (bf16[640,256,128]{2,1,0:T(8,128)(2,1)}, ...), branch_computations={%region_0.0_spmd, %region_1.0_spmd, %region_2.0_spmd, %region_3.0_... | conditional | bytes 8 | solution.py:537
  21.7 198.4 %exchange_near.9 = (bf16[1536,256,128]{2,1,0:T(8,128)(2,1)}, bf16[74,256,128]{2,1,0:T(8,128)(2,1)S(1)}) custom-call(bf16[640,256,128]{2,1,0:T(8,128)(2,1)} %get-tuple-element.77.refs_0_, bf16[256,256,128]{2,1,0:T(8,128)(2,1)} %get-tuple-element.78.refs_1_, bf16[8,256,128]{2,1,0:T(8,128)(2,1)S(1)} %get-tuple-element.79.refs_2_), custom_call_target="tpu_custom_call" | custom-call | tf_op jit(solution)/shard_map/cond/branch_2_fun/exchange_near/pallas_call | solution.py:524
  220.1 5.6 %pack_relay.9.refs_0_ = bf16[896,256,128]{2,1,0:T(8,128)(2,1)} custom-call(s32[40,256]{1,0:T(8,128)S(1)} %get-tuple-element.76.plan, bf16[74,256,128]{2,1,0:T(8,128)(2,1)S(1)} %get-tuple-element.80.arrived), custom_call_target="tpu_custom_call" | custom-call | tf_op jit(solution)/shard_map/cond/branch_2_fun/pack_relay/pallas_call | solution.py:526
  225.7 116.6 %exchange_far.9 = bf16[1536,256,128]{2,1,0:T(8,128)(2,1)} custom-call(bf16[896,256,128]{2,1,0:T(8,128)(2,1)} %pack_relay.9.refs_0_, bf16[1536,256,128]{2,1,0:T(8,128)(2,1)} %get-tuple-element.81.refs_1_), custom_call_target="tpu_custom_call", output_to_operand_aliasing={{}: (1, {})} | custom-call | tf_op jit(solution)/shard_map/cond/branch_2_fun/exchange_far/pallas_call | solution.py:534
  342.3 31.2 %attend.1 = bf16[8,1024,128]{2,1,0:T(8,128)(2,1)} custom-call(s32[40,256]{1,0:T(8,128)S(1)} %get-tuple-element.115.plan, bf16[8,1024,128]{2,1,0:T(8,128)(2,1)} %bitcast.19, bf16[8,256,128]{2,1,0:T(8,128)(2,1)} %bitcast.16, bf16[8,256,128]{2,1,0:T(8,128)(2,1)} %bitcast.18, bf16[1536,256,128]{2,1,0:T(8,128)(2,1)} %get-tuple-element.121.recv), custom_call_target="tpu_custom_call" | custom-call | tf_op jit(solution)/shard_map/attend/pallas_call | solution.py:542

commit v6 on v5

--- a/solution.py
+++ b/solution.py
@@ -10,7 +10,7 @@
 F32 = jnp.float32
 BF16 = jnp.bfloat16
 ROW_CAP = 5
-FIND_STEP = 4
+FIND_STEP = 8
 PIECE = 32
 HOT_CAP = 64
 PLANES = 4
@@ -331,6 +331,9 @@
             sends.append((to * n_cols + col, hot_for(to), hot_here))
         own_copies.append((hot_for(plane), own.at[pl.ds(pair_send, HOT_PART)], hot_here))
 
+    if first:
+        near, cross, hots = sends[:n_half - 1], sends[n_half - 1:n_half], sends[n_half:]
+        sends = near[:8] + cross + hots + near[8:]
     barrier = pltpu.get_barrier_semaphore()
     for peer, _, _ in sends:
         pl.semaphore_signal(barrier, inc=1, device_id=(peer,), device_id_type=MESH)
@@ -436,7 +439,8 @@
             probabilities(h - 1, 1 - at)
             values(h - 2, at)
         return carry
-    lax.fori_loop(1, kv_heads // 2, steady, 0)
+    for pair in range(1, kv_heads // 2):
+        steady(pair, 0)
     probabilities(kv_heads - 1, 1)
     values(kv_heads - 2, 0)
     values(kv_heads - 1, 1)

time: 373 us -> 368 us (0.987)
  Pallas kernels: 372 us -> 366 us
    pallas_call x1, Pallas kernels: 31.2 us -> 26.7 us  [local_step(): pl.pallas_call(functools.partial(attend_kernel, cfg), out_shape=jax.Shape...]
where the time goes in v6:
time: 368 us
  Pallas kernels  366 us (99%)
    pallas_call x1, Pallas kernels, exchange(): exchange_call(True, near_send, (shaped(n_recv), shaped(n_arrived)), 3, {}...  195 us
    pallas_call x1, Pallas kernels, exchange(): exchange_call(False, far_send, shaped(n_recv), 2, {1: 0}, 'exchange_far')  119 us
    pallas_call x1, Pallas kernels, local_step(): pl.pallas_call(functools.partial(attend_kernel, cfg), out_shape=jax.Shape...  26.7 us
    pallas_call x1, Pallas kernels, local_step(): pl.pallas_call(functools.partial(plan_kernel, (n_dev, n_half, per_dev, pa...  19.4 us

profile of v6, /device:TPU:0, one launch (start us, length us, event | category | flops | bytes accessed | tf_op | source)
XLA Modules:
  0.0 368.0 jit_solution(17312742475906100611)
XLA Ops:
  0.6 19.4 %plan.1 = (s32[40,256]{1,0:T(8,128)S(1)}, bf16[640,256,128]{2,1,0:T(8,128)(2,1)}, bf16[256,256,128]{2,1,0:T(8,128)(2,1)}, bf16[8,256,128]{2,1,0:T(8,128)(2,1)S(1...) custom-call(s32[2,8]{1,0:T(2,128)} %bitcast.22, s32[64,256]{1,0:T(8,128)} %bitcast.21, ...), custom_call_target="tpu_custom_call" | custom-call | tf_op jit(solution)/shard_map/plan/pallas_call | solution.py:478
  20.0 0.5 slice.3
  21.2 319.9 %conditional.1 = (bf16[1536,256,128]{2,1,0:T(8,128)(2,1)}) conditional(s32[]{:T(128)} %bitcast.9, (bf16[640,256,128]{2,1,0:T(8,128)(2,1)}, bf16[256,256,128]{2,1,0:T(8,128)(2,1)}, bf16[8,256,128]{2,1,0:T(8,128)(2,1)S(1)}, s32[40,256]{1,0:T(8,128)S(1)}) %tuple.29, (bf16[640,256,128]{2,1,0:T(8,128)(2,1)}, ...), branch_computations={%region_0.0_spmd, %region_1.0_spmd, %region_2.0_spmd, %region_3.0_... | conditional | bytes 8 | solution.py:541
  21.2 195.2 %exchange_near.9 = (bf16[1536,256,128]{2,1,0:T(8,128)(2,1)}, bf16[74,256,128]{2,1,0:T(8,128)(2,1)S(1)}) custom-call(bf16[640,256,128]{2,1,0:T(8,128)(2,1)} %get-tuple-element.77.refs_0_, bf16[256,256,128]{2,1,0:T(8,128)(2,1)} %get-tuple-element.78.refs_1_, bf16[8,256,128]{2,1,0:T(8,128)(2,1)S(1)} %get-tuple-element.79.refs_2_), custom_call_target="tpu_custom_call" | custom-call | tf_op jit(solution)/shard_map/cond/branch_2_fun/exchange_near/pallas_call | solution.py:528
  216.4 5.6 %pack_relay.9.refs_0_ = bf16[896,256,128]{2,1,0:T(8,128)(2,1)} custom-call(s32[40,256]{1,0:T(8,128)S(1)} %get-tuple-element.76.plan, bf16[74,256,128]{2,1,0:T(8,128)(2,1)S(1)} %get-tuple-element.80.arrived), custom_call_target="tpu_custom_call" | custom-call | tf_op jit(solution)/shard_map/cond/branch_2_fun/pack_relay/pallas_call | solution.py:530
  222.0 119.0 %exchange_far.9 = bf16[1536,256,128]{2,1,0:T(8,128)(2,1)} custom-call(bf16[896,256,128]{2,1,0:T(8,128)(2,1)} %pack_relay.9.refs_0_, bf16[1536,256,128]{2,1,0:T(8,128)(2,1)} %get-tuple-element.81.refs_1_), custom_call_target="tpu_custom_call", output_to_operand_aliasing={{}: (1, {})} | custom-call | tf_op jit(solution)/shard_map/cond/branch_2_fun/exchange_far/pallas_call | solution.py:538
  341.1 26.7 %attend.1 = bf16[8,1024,128]{2,1,0:T(8,128)(2,1)} custom-call(s32[40,256]{1,0:T(8,128)S(1)} %get-tuple-element.115.plan, bf16[8,1024,128]{2,1,0:T(8,128)(2,1)} %bitcast.19, bf16[8,256,128]{2,1,0:T(8,128)(2,1)} %bitcast.16, bf16[8,256,128]{2,1,0:T(8,128)(2,1)} %bitcast.18, bf16[1536,256,128]{2,1,0:T(8,128)(2,1)} %get-tuple-element.121.recv), custom_call_target="tpu_custom_call" | custom-call | tf_op jit(solution)/shard_map/attend/pallas_call | solution.py:546
